TPU v7x, 256 devices: a whole 4x4x8 slice. The times are simulated.
256 devices in a mesh: space: 64 (over z, y, core), slab: 4 (over x).
Axes of the slice: x: 4, y: 4, z: 8, core: 2. Of those that a mesh axis runs over, the one named last changes fastest.
Arguments:
- source: float32 [4, 256, 16384], P('slab', None, 'space'), may hold values from -6 to 6
- initial: float32 [64, 16384], P(None, 'space'), may hold values from -6 to 6
- inverse: float32 [256, 256], replicated, may hold values from -0.1 to 0.7, as said below
- lift: float32 [256, 384], replicated, may hold values from -0.109375 to 0.109375
- lift_time: float32 [256, 64], replicated, may hold values from -0.375 to 0.375
- links: int32 [6, 16384], P(None, 'space'), may hold values from 0 to 1791, as said below
- orient: int32 [6, 16384], P(None, 'space'), may hold values from 0 to 7
- exports: int32 [16384], P('space'), may hold values from 0 to 1535, as said below
- counts: int32 [64], P('space'), may hold values from 128 to 256, as said below
Outputs:
- state: float32 [4, 256, 16384], P('slab', None, 'space')
Inputs may be any that keep to these rules, and one draw needn't show every extreme that they name: `links`: a value below 1536 is f*256 + e naming face f of a live slot e of the same partition; others are 1536 + m naming slot m of the imported neighbour traces. `exports`: each value is f*256 + e with e a live slot of that partition. `counts`: some partition holds exactly 256. `inverse`: full rank; diagonal entries between 0.5 and 0.7, off-diagonal entries of magnitude at most 0.1.
All inputs are finite; a program needn't handle non-finite values.
Results may differ from a plain program's by a relative error of at most 0.0001.
Values sent between devices are 32-bit elements; how exact they have to be, the bound alone decides.
A program may use at most 64 MiB of HBM per device.

v0:
```python
import jax
import jax.numpy as jnp
from jax import lax
from jax.sharding import PartitionSpec as P

ITERS = 6


def with_halo(block, sides, width):
    for axis, dim in sides:
        count = lax.axis_size(axis)
        forward = [(i, i + 1) for i in range(count - 1)]
        forward.append((count - 1, 0))
        backward = [(target, source) for source, target in forward]
        low = lax.ppermute(
            lax.slice_in_dim(block, block.shape[dim] - width, None, axis=dim), axis, forward
        )
        high = lax.ppermute(lax.slice_in_dim(block, 0, width, axis=dim), axis, backward)
        block = jnp.concatenate([low, block, high], axis=dim)
    return block


def shifted(block, axis, distance):
    devices = range(lax.axis_size(axis))
    route = [(i - distance, i) for i in devices if i - distance in devices]
    return lax.ppermute(block, axis, route)


def face_stack(volume, axis):
    pieces = [
        volume[:, 0],
        volume[:, 3],
        volume[:, :, 0],
        volume[:, :, 3],
        volume[:, :, :, 0],
        volume[:, :, :, 3],
    ]
    return jnp.stack(pieces, axis=axis)


def orient_traces(values, turn):
    swapped = jnp.swapaxes(values, 1, 2)
    values = jnp.where(jnp.bitwise_and(turn, 4) > 0, swapped, values)
    values = jnp.where(jnp.bitwise_and(turn, 1) > 0, jnp.flip(values, 1), values)
    values = jnp.where(jnp.bitwise_and(turn, 2) > 0, jnp.flip(values, 2), values)
    return values


def body(source, initial, inverse, lift, lift_time, links, orient, exports, counts):
    highest = lax.Precision.HIGHEST
    elems = links.shape[1]
    peer = exports.shape[0] // 2
    local_width = 6 * elems
    live = (jnp.arange(elems, dtype=jnp.int32) < counts[0]).astype(jnp.float32)[None, :]
    flat_links = links.reshape(-1)
    first_slab = lax.axis_index("slab") == 0
    state = jnp.zeros((256, elems), jnp.float32)
    for step in range(ITERS):
        traces = face_stack(state.reshape(4, 4, 4, 4, elems), 3).reshape(64, local_width)
        outgoing = jnp.take(traces, exports, axis=1)
        extended = with_halo(outgoing, (("space", 1),), peer)
        table = jnp.concatenate([traces, extended[:, :peer], extended[:, 3 * peer :]], axis=1)
        gathered = jnp.take(table, flat_links, axis=1)
        nbr = orient_traces(gathered.reshape(4, 4, 4, 6, elems), orient).reshape(384, elems)
        top = state[192:]
        arrived = shifted(top, "slab", 1)
        top_in = jnp.where(first_slab, initial, arrived)
        time_term = jnp.dot(lift_time, top_in, precision=highest)
        rhs = source[0] + jnp.dot(lift, nbr, precision=highest) + time_term
        state = jnp.dot(inverse, rhs, precision=highest) * live
    return state[None]


def solution(mesh):
    return jax.shard_map(
        body,
        mesh=mesh,
        in_specs=(
            P("slab", None, "space"),
            P(None, "space"),
            P(),
            P(),
            P(),
            P(None, "space"),
            P(None, "space"),
            P("space"),
            P("space"),
        ),
        out_specs=P("slab", None, "space"),
        check_vma=False,
    )
```

profile of v0, /device:TPU:121, one launch (start us, length us, event | category | flops | bytes accessed | tf_op | source)
XLA Modules:
  0.0 98.0 jit_solution(6730955618159573962)
XLA Ops:
  0.0 3.2 %collective-permute-start.2 = (f32[64,256]{1,0:T(8,128)S(1)}, f32[64,256]{1,0:T(8,128)S(1)}, u32[]{:S(2)}, u32[]{:S(2)}) collective-permute-start(f32[64,256]{1,0:T(8,128)S(1)} %slice.146), channel_id=1, source_target_pairs={{0,1},{1,2},{2,3},{4,5},{5,6},{6,7},{8,9},{9,10},{10,11},{12,13},{... | collective-permute-start | bytes 196616 | tf_op jit(solution)/shard_map/ppermute | solution.py:26
  3.7 0.7 gather_fusion
  4.6 3.4 %collective-permute-start = (f32[64,128]{0,1:T(8,128)S(1)}, f32[64,128]{0,1:T(8,128)S(1)}, u32[]{:S(2)}, u32[]{:S(2)}) collective-permute-start(f32[64,128]{0,1:T(8,128)S(1)} %get-tuple-element.47), channel_id=1, source_target_pairs={{0,4},{4,8},{8,12},{12,16},{16,20},{20,24},{24,28},{28,32},{32,36}... | collective-permute-start | bytes 98312 | tf_op jit(solution)/shard_map/ppermute | solution.py:15
  9.3 5.7 %collective-permute-done.1 = f32[64,128]{0,1:T(8,128)S(1)} collective-permute-done((f32[64,128]{0,1:T(8,128)S(1)}, f32[64,128]{0,1:T(8,128)S(1)}, u32[]{:S(2)}, u32[]{:S(2)}) %collective-permute-start.1) | collective-permute-done | bytes 32800 | tf_op jit(solution)/shard_map/ppermute | solution.py:18
  15.1 2.6 %gather_fusion.1 = f32[1536,64]{1,0:T(8,128)S(1)} fusion(f32[64,1792]{0,1:T(8,128)S(1)} %pad_maximum_fusion, s32[2048]{0:T(1024)S(1)} %pad_clamp_fusion), kind=kCustom, calls=%fused_computation.1.clone | custom fusion | bytes 792576 | tf_op jit(solution)/shard_map/jit(_take)/gather | solution.py:63
  18.6 0.9 copy-done.1
  21.9 0.6 stack.33
  23.0 0.7 gather_fusion.2
  24.4 3.1 %collective-permute-start.5 = (f32[64,256]{1,0:T(8,128)S(1)}, f32[64,256]{1,0:T(8,128)S(1)}, u32[]{:S(2)}, u32[]{:S(2)}) collective-permute-start(f32[64,256]{1,0:T(8,128)S(1)} %slice.226), channel_id=1, source_target_pairs={{0,1},{1,2},{2,3},{4,5},{5,6},{6,7},{8,9},{9,10},{10,11},{12,13},{... | collective-permute-start | bytes 196616 | tf_op jit(solution)/shard_map/ppermute | solution.py:26
  27.6 3.5 %collective-permute-done.4 = f32[64,128]{0,1:T(8,128)S(1)} collective-permute-done((f32[64,128]{0,1:T(8,128)S(1)}, f32[64,128]{0,1:T(8,128)S(1)}, u32[]{:S(2)}, u32[]{:S(2)}) %collective-permute-start.4) | collective-permute-done | bytes 32800 | tf_op jit(solution)/shard_map/ppermute | solution.py:18
  31.1 2.6 %gather_fusion.3 = f32[1536,64]{1,0:T(8,128)S(1)} fusion(f32[64,1792]{0,1:T(8,128)S(1)} %pad_maximum_fusion.1, s32[2048]{0:T(1024)S(1)} %pad_clamp_fusion), kind=kCustom, calls=%fused_computation.7.clone | custom fusion | bytes 792576 | tf_op jit(solution)/shard_map/jit(_take)/gather | solution.py:63
  36.5 0.6 stack.34
  37.6 0.7 gather_fusion.4
  38.5 1.6 %collective-permute-start.6 = (f32[64,128]{0,1:T(8,128)S(1)}, f32[64,128]{0,1:T(8,128)S(1)}, u32[]{:S(2)}, u32[]{:S(2)}) collective-permute-start(f32[64,128]{0,1:T(8,128)S(1)} %get-tuple-element.43), channel_id=1, source_target_pairs={{0,4},{4,8},{8,12},{12,16},{16,20},{20,24},{24,28},{28,32},{32,36}... | collective-permute-start | bytes 98312 | tf_op jit(solution)/shard_map/ppermute | solution.py:15
  40.0 2.8 %collective-permute-start.8 = (f32[64,256]{1,0:T(8,128)S(1)}, f32[64,256]{1,0:T(8,128)S(1)}, u32[]{:S(2)}, u32[]{:S(2)}) collective-permute-start(f32[64,256]{1,0:T(8,128)S(1)} %slice.235), channel_id=1, source_target_pairs={{0,1},{1,2},{2,3},{4,5},{5,6},{6,7},{8,9},{9,10},{10,11},{12,13},{... | collective-permute-start | bytes 196616 | tf_op jit(solution)/shard_map/ppermute | solution.py:26
  42.9 4.2 %collective-permute-done.7 = f32[64,128]{0,1:T(8,128)S(1)} collective-permute-done((f32[64,128]{0,1:T(8,128)S(1)}, f32[64,128]{0,1:T(8,128)S(1)}, u32[]{:S(2)}, u32[]{:S(2)}) %collective-permute-start.7) | collective-permute-done | bytes 32800 | tf_op jit(solution)/shard_map/ppermute | solution.py:18
  47.1 2.6 %gather_fusion.5 = f32[1536,64]{1,0:T(8,128)S(1)} fusion(f32[64,1792]{0,1:T(8,128)S(1)} %pad_maximum_fusion.2, s32[2048]{0:T(1024)S(1)} %pad_clamp_fusion), kind=kCustom, calls=%fused_computation.8.clone | custom fusion | bytes 792576 | tf_op jit(solution)/shard_map/jit(_take)/gather | solution.py:63
  53.6 0.7 gather_fusion.6
  54.5 1.3 %collective-permute-start.9 = (f32[64,128]{0,1:T(8,128)S(1)}, f32[64,128]{0,1:T(8,128)S(1)}, u32[]{:S(2)}, u32[]{:S(2)}) collective-permute-start(f32[64,128]{0,1:T(8,128)S(1)} %get-tuple-element.41), channel_id=1, source_target_pairs={{0,4},{4,8},{8,12},{12,16},{16,20},{20,24},{24,28},{28,32},{32,36}... | collective-permute-start | bytes 98312 | tf_op jit(solution)/shard_map/ppermute | solution.py:15
  55.7 2.1 %collective-permute-start.11 = (f32[64,256]{1,0:T(8,128)S(1)}, f32[64,256]{1,0:T(8,128)S(1)}, u32[]{:S(2)}, u32[]{:S(2)}) collective-permute-start(f32[64,256]{1,0:T(8,128)S(1)} %slice.244), channel_id=1, source_target_pairs={{0,1},{1,2},{2,3},{4,5},{5,6},{6,7},{8,9},{9,10},{10,11},{12,13},{... | collective-permute-start | bytes 196616 | tf_op jit(solution)/shard_map/ppermute | solution.py:26
  57.9 4.8 %collective-permute-done.10 = f32[64,128]{0,1:T(8,128)S(1)} collective-permute-done((f32[64,128]{0,1:T(8,128)S(1)}, f32[64,128]{0,1:T(8,128)S(1)}, u32[]{:S(2)}, u32[]{:S(2)}) %collective-permute-start.10) | collective-permute-done | bytes 32800 | tf_op jit(solution)/shard_map/ppermute | solution.py:18
  62.8 2.6 %gather_fusion.7 = f32[1536,64]{1,0:T(8,128)S(1)} fusion(f32[64,1792]{0,1:T(8,128)S(1)} %pad_maximum_fusion.3, s32[2048]{0:T(1024)S(1)} %pad_clamp_fusion), kind=kCustom, calls=%fused_computation.9.clone | custom fusion | bytes 792576 | tf_op jit(solution)/shard_map/jit(_take)/gather | solution.py:63
  68.3 0.6 stack.36
  69.3 0.7 gather_fusion.8
  70.8 2.1 %collective-permute-start.14 = (f32[64,256]{1,0:T(8,128)S(1)}, f32[64,256]{1,0:T(8,128)S(1)}, u32[]{:S(2)}, u32[]{:S(2)}) collective-permute-start(f32[64,256]{1,0:T(8,128)S(1)} %slice.253), channel_id=1, source_target_pairs={{0,1},{1,2},{2,3},{4,5},{5,6},{6,7},{8,9},{9,10},{10,11},{12,13},{... | collective-permute-start | bytes 196616 | tf_op jit(solution)/shard_map/ppermute | solution.py:26
  72.9 4.6 %collective-permute-done.13 = f32[64,128]{0,1:T(8,128)S(1)} collective-permute-done((f32[64,128]{0,1:T(8,128)S(1)}, f32[64,128]{0,1:T(8,128)S(1)}, u32[]{:S(2)}, u32[]{:S(2)}) %collective-permute-start.13) | collective-permute-done | bytes 32800 | tf_op jit(solution)/shard_map/ppermute | solution.py:18
  77.6 2.6 %gather_fusion.9 = f32[1536,64]{1,0:T(8,128)S(1)} fusion(f32[64,1792]{0,1:T(8,128)S(1)} %pad_maximum_fusion.4, s32[2048]{0:T(1024)S(1)} %pad_clamp_fusion), kind=kCustom, calls=%fused_computation.10.clone | custom fusion | bytes 792576 | tf_op jit(solution)/shard_map/jit(_take)/gather | solution.py:63
  84.1 0.7 gather_fusion.10
  85.6 1.7 %collective-permute-start.17 = (f32[64,256]{1,0:T(8,128)S(1)}, f32[64,256]{1,0:T(8,128)S(1)}, u32[]{:S(2)}, u32[]{:S(2)}) collective-permute-start(f32[64,256]{1,0:T(8,128)S(1)} %slice.262), channel_id=1, source_target_pairs={{0,1},{1,2},{2,3},{4,5},{5,6},{6,7},{8,9},{9,10},{10,11},{12,13},{... | collective-permute-start | bytes 196616 | tf_op jit(solution)/shard_map/ppermute | solution.py:26
  87.3 5.1 %collective-permute-done.16 = f32[64,128]{0,1:T(8,128)S(1)} collective-permute-done((f32[64,128]{0,1:T(8,128)S(1)}, f32[64,128]{0,1:T(8,128)S(1)}, u32[]{:S(2)}, u32[]{:S(2)}) %collective-permute-start.16) | collective-permute-done | bytes 32800 | tf_op jit(solution)/shard_map/ppermute | solution.py:18
  92.4 2.6 %gather_fusion.11 = f32[1536,64]{1,0:T(8,128)S(1)} fusion(f32[64,1792]{0,1:T(8,128)S(1)} %pad_maximum_fusion.5, s32[2048]{0:T(1024)S(1)} %pad_clamp_fusion), kind=kCustom, calls=%fused_computation.11.clone | custom fusion | bytes 792576 | tf_op jit(solution)/shard_map/jit(_take)/gather | solution.py:63
  96.9 1.1 %fusion = f32[1,256,256]{2,1,0:T(8,128)} fusion(f32[256,256]{1,0:T(8,128)S(1)} %fusion.12, f32[256,256]{1,0:T(8,128)S(1)} %copy-done.2, f32[256]{0:T(256)S(1)} %compare_convert_fusion), kind=kOutput, calls=%fused_computation.13 | convolution fusion | flops 201392128 | bytes 787456 | tf_op jit(solution)/shard_map/dot_general | solution.py:70
  (185 shorter events, 22.9 us)
Async XLA Ops:
  0.0 18.5 %copy-start = (f32[256,384]{1,0:T(8,128)S(1)}, f32[256,384]{1,0:T(8,128)}, u32[]{:S(2)}) copy-start(f32[256,384]{1,0:T(8,128)} %param.16) | copy-start | bytes 1179652
  0.0 3.3 %copy-start.7 = (s32[256]{0:T(256)S(1)}, s32[256]{0:T(256)}, u32[]{:S(2)}) copy-start(s32[256]{0:T(256)} %param.20) | copy-start | bytes 3076
  0.0 20.0 %collective-permute-start.2 = (f32[64,256]{1,0:T(8,128)S(1)}, f32[64,256]{1,0:T(8,128)S(1)}, u32[]{:S(2)}, u32[]{:S(2)}) collective-permute-start(f32[64,256]{1,0:T(8,128)S(1)} %slice.146), channel_id=1, source_target_pairs={{0,1},{1,2},{2,3},{4,5},{5,6},{6,7},{8,9},{9,10},{10,11},{12,13},{... | collective-permute-start | bytes 196616 | tf_op jit(solution)/shard_map/ppermute | solution.py:26
  4.5 3.5 %copy-start.6 = (s32[6,256]{1,0:T(8,128)S(1)}, s32[6,256]{1,0:T(8,128)}, u32[]{:S(2)}) copy-start(s32[6,256]{1,0:T(8,128)} %param.18) | copy-start | bytes 18436
  4.6 4.8 %collective-permute-start = (f32[64,128]{0,1:T(8,128)S(1)}, f32[64,128]{0,1:T(8,128)S(1)}, u32[]{:S(2)}, u32[]{:S(2)}) collective-permute-start(f32[64,128]{0,1:T(8,128)S(1)} %get-tuple-element.47), channel_id=1, source_target_pairs={{0,4},{4,8},{8,12},{12,16},{16,20},{20,24},{24,28},{28,32},{32,36}... | collective-permute-start | bytes 98312 | tf_op jit(solution)/shard_map/ppermute | solution.py:15
  8.0 7.0 %collective-permute-start.1 = (f32[64,128]{0,1:T(8,128)S(1)}, f32[64,128]{0,1:T(8,128)S(1)}, u32[]{:S(2)}, u32[]{:S(2)}) collective-permute-start(f32[64,128]{0,1:T(8,128)S(1)} %get-tuple-element.48), channel_id=1, source_target_pairs={{4,0},{8,4},{12,8},{16,12},{20,16},{24,20},{28,24},{32,28},{36,32}... | collective-permute-start | bytes 98312 | tf_op jit(solution)/shard_map/ppermute | solution.py:18
  8.0 0.7 copy-start.5
  18.5 1.0 copy-start.1
  19.4 0.8 copy-start.3
  19.4 0.9 copy-start.4
  20.0 1.0 copy-start.2
  23.9 3.7 %collective-permute-start.3 = (f32[64,128]{0,1:T(8,128)S(1)}, f32[64,128]{0,1:T(8,128)S(1)}, u32[]{:S(2)}, u32[]{:S(2)}) collective-permute-start(f32[64,128]{0,1:T(8,128)S(1)} %get-tuple-element.45), channel_id=1, source_target_pairs={{0,4},{4,8},{8,12},{12,16},{16,20},{20,24},{24,28},{28,32},{32,36}... | collective-permute-start | bytes 98312 | tf_op jit(solution)/shard_map/ppermute | solution.py:15
  23.9 7.1 %collective-permute-start.4 = (f32[64,128]{0,1:T(8,128)S(1)}, f32[64,128]{0,1:T(8,128)S(1)}, u32[]{:S(2)}, u32[]{:S(2)}) collective-permute-start(f32[64,128]{0,1:T(8,128)S(1)} %get-tuple-element.46), channel_id=1, source_target_pairs={{4,0},{8,4},{12,8},{16,12},{20,16},{24,20},{28,24},{32,28},{36,32}... | collective-permute-start | bytes 98312 | tf_op jit(solution)/shard_map/ppermute | solution.py:18
  24.4 10.7 %collective-permute-start.5 = (f32[64,256]{1,0:T(8,128)S(1)}, f32[64,256]{1,0:T(8,128)S(1)}, u32[]{:S(2)}, u32[]{:S(2)}) collective-permute-start(f32[64,256]{1,0:T(8,128)S(1)} %slice.226), channel_id=1, source_target_pairs={{0,1},{1,2},{2,3},{4,5},{5,6},{6,7},{8,9},{9,10},{10,11},{12,13},{... | collective-permute-start | bytes 196616 | tf_op jit(solution)/shard_map/ppermute | solution.py:26
  38.5 4.4 %collective-permute-start.6 = (f32[64,128]{0,1:T(8,128)S(1)}, f32[64,128]{0,1:T(8,128)S(1)}, u32[]{:S(2)}, u32[]{:S(2)}) collective-permute-start(f32[64,128]{0,1:T(8,128)S(1)} %get-tuple-element.43), channel_id=1, source_target_pairs={{0,4},{4,8},{8,12},{12,16},{16,20},{20,24},{24,28},{28,32},{32,36}... | collective-permute-start | bytes 98312 | tf_op jit(solution)/shard_map/ppermute | solution.py:15
  40.0 7.0 %collective-permute-start.7 = (f32[64,128]{0,1:T(8,128)S(1)}, f32[64,128]{0,1:T(8,128)S(1)}, u32[]{:S(2)}, u32[]{:S(2)}) collective-permute-start(f32[64,128]{0,1:T(8,128)S(1)} %get-tuple-element.44), channel_id=1, source_target_pairs={{4,0},{8,4},{12,8},{16,12},{20,16},{24,20},{28,24},{32,28},{36,32}... | collective-permute-start | bytes 98312 | tf_op jit(solution)/shard_map/ppermute | solution.py:18
  40.0 11.1 %collective-permute-start.8 = (f32[64,256]{1,0:T(8,128)S(1)}, f32[64,256]{1,0:T(8,128)S(1)}, u32[]{:S(2)}, u32[]{:S(2)}) collective-permute-start(f32[64,256]{1,0:T(8,128)S(1)} %slice.235), channel_id=1, source_target_pairs={{0,1},{1,2},{2,3},{4,5},{5,6},{6,7},{8,9},{9,10},{10,11},{12,13},{... | collective-permute-start | bytes 196616 | tf_op jit(solution)/shard_map/ppermute | solution.py:26
  54.5 3.4 %collective-permute-start.9 = (f32[64,128]{0,1:T(8,128)S(1)}, f32[64,128]{0,1:T(8,128)S(1)}, u32[]{:S(2)}, u32[]{:S(2)}) collective-permute-start(f32[64,128]{0,1:T(8,128)S(1)} %get-tuple-element.41), channel_id=1, source_target_pairs={{0,4},{4,8},{8,12},{12,16},{16,20},{20,24},{24,28},{28,32},{32,36}... | collective-permute-start | bytes 98312 | tf_op jit(solution)/shard_map/ppermute | solution.py:15
  55.7 7.0 %collective-permute-start.10 = (f32[64,128]{0,1:T(8,128)S(1)}, f32[64,128]{0,1:T(8,128)S(1)}, u32[]{:S(2)}, u32[]{:S(2)}) collective-permute-start(f32[64,128]{0,1:T(8,128)S(1)} %get-tuple-element.42), channel_id=1, source_target_pairs={{4,0},{8,4},{12,8},{16,12},{20,16},{24,20},{28,24},{32,28},{36,32}... | collective-permute-start | bytes 98312 | tf_op jit(solution)/shard_map/ppermute | solution.py:18
  55.7 11.1 %collective-permute-start.11 = (f32[64,256]{1,0:T(8,128)S(1)}, f32[64,256]{1,0:T(8,128)S(1)}, u32[]{:S(2)}, u32[]{:S(2)}) collective-permute-start(f32[64,256]{1,0:T(8,128)S(1)} %slice.244), channel_id=1, source_target_pairs={{0,1},{1,2},{2,3},{4,5},{5,6},{6,7},{8,9},{9,10},{10,11},{12,13},{... | collective-permute-start | bytes 196616 | tf_op jit(solution)/shard_map/ppermute | solution.py:26
  70.2 2.7 %collective-permute-start.12 = (f32[64,128]{0,1:T(8,128)S(1)}, f32[64,128]{0,1:T(8,128)S(1)}, u32[]{:S(2)}, u32[]{:S(2)}) collective-permute-start(f32[64,128]{0,1:T(8,128)S(1)} %get-tuple-element.39), channel_id=1, source_target_pairs={{0,4},{4,8},{8,12},{12,16},{16,20},{20,24},{24,28},{28,32},{32,36}... | collective-permute-start | bytes 98312 | tf_op jit(solution)/shard_map/ppermute | solution.py:15
  70.5 7.0 %collective-permute-start.13 = (f32[64,128]{0,1:T(8,128)S(1)}, f32[64,128]{0,1:T(8,128)S(1)}, u32[]{:S(2)}, u32[]{:S(2)}) collective-permute-start(f32[64,128]{0,1:T(8,128)S(1)} %get-tuple-element.40), channel_id=1, source_target_pairs={{4,0},{8,4},{12,8},{16,12},{20,16},{24,20},{28,24},{32,28},{36,32}... | collective-permute-start | bytes 98312 | tf_op jit(solution)/shard_map/ppermute | solution.py:18
  70.8 10.9 %collective-permute-start.14 = (f32[64,256]{1,0:T(8,128)S(1)}, f32[64,256]{1,0:T(8,128)S(1)}, u32[]{:S(2)}, u32[]{:S(2)}) collective-permute-start(f32[64,256]{1,0:T(8,128)S(1)} %slice.253), channel_id=1, source_target_pairs={{0,1},{1,2},{2,3},{4,5},{5,6},{6,7},{8,9},{9,10},{10,11},{12,13},{... | collective-permute-start | bytes 196616 | tf_op jit(solution)/shard_map/ppermute | solution.py:26
  85.0 2.3 %collective-permute-start.15 = (f32[64,128]{0,1:T(8,128)S(1)}, f32[64,128]{0,1:T(8,128)S(1)}, u32[]{:S(2)}, u32[]{:S(2)}) collective-permute-start(f32[64,128]{0,1:T(8,128)S(1)} %get-tuple-element.37), channel_id=1, source_target_pairs={{0,4},{4,8},{8,12},{12,16},{16,20},{20,24},{24,28},{28,32},{32,36}... | collective-permute-start | bytes 98312 | tf_op jit(solution)/shard_map/ppermute | solution.py:15
  85.4 7.0 %collective-permute-start.16 = (f32[64,128]{0,1:T(8,128)S(1)}, f32[64,128]{0,1:T(8,128)S(1)}, u32[]{:S(2)}, u32[]{:S(2)}) collective-permute-start(f32[64,128]{0,1:T(8,128)S(1)} %get-tuple-element.38), channel_id=1, source_target_pairs={{4,0},{8,4},{12,8},{16,12},{20,16},{24,20},{28,24},{32,28},{36,32}... | collective-permute-start | bytes 98312 | tf_op jit(solution)/shard_map/ppermute | solution.py:18
  85.6 10.9 %collective-permute-start.17 = (f32[64,256]{1,0:T(8,128)S(1)}, f32[64,256]{1,0:T(8,128)S(1)}, u32[]{:S(2)}, u32[]{:S(2)}) collective-permute-start(f32[64,256]{1,0:T(8,128)S(1)} %slice.262), channel_id=1, source_target_pairs={{0,1},{1,2},{2,3},{4,5},{5,6},{6,7},{8,9},{9,10},{10,11},{12,13},{... | collective-permute-start | bytes 196616 | tf_op jit(solution)/shard_map/ppermute | solution.py:26
where the time goes:
time: 98.4 us; the launch traced here: 98 us
  local copies, waits for them, and re-layouts  31.9 us (32%)
  waiting for transfers between devices  28.5 us (29%)
  starting transfers between devices  23.2 us (24%)
  matrix products  9.2 us (9%)
  other arithmetic  3.37 us (3%)
  between operations  2 us (2%)
    ppermute x6, waiting for transfers between devices, with_halo(): lax.ppermute(lax.slice_in_dim(block, 0, width, axis=dim), axis, backward)  27.8 us
    gather x6, local copies, waits for them, and re-layouts, body(): gathered = jnp.take(table, flat_links, axis=1)  15.6 us
    ppermute x6, starting transfers between devices, shifted(): return lax.ppermute(block, axis, route)  15.1 us
    ppermute x6, starting transfers between devices, with_halo(): lax.ppermute(lax.slice_in_dim(block, block.shape[dim] - width, None, axis...  7.07 us
    another operation x40, local copies, waits for them, and re-layouts, face_stack(): return jnp.stack(pieces, axis=axis)  5.04 us
    gather x6, local copies, waits for them, and re-layouts, body(): outgoing = jnp.take(traces, exports, axis=1)  4.41 us
    dot_general x6, matrix products, body(): rhs = source[0] + jnp.dot(lift, nbr, precision=highest) + time_term  3.58 us
    dot_general x6, matrix products, body(): state = jnp.dot(inverse, rhs, precision=highest) * live  3.09 us
  transfers between devices with their start and end apart: 18, of which 7 were waited for; matrix products, arithmetic and copies ran while one was open for 26% of the time, Pallas kernels for 0%

commit v1 on v0

v1 whole, which is shorter than its diff:
```python
import functools

import jax
import jax.numpy as jnp
from jax import lax
from jax.experimental import pallas as pl
from jax.experimental.pallas import tpu as pltpu
from jax.sharding import PartitionSpec as P

ROUNDS = 5
E = 256
PEER = 128
LOCAL = 6 * E
TABLE = LOCAL + 2 * PEER
K = 6 * 128 + 128
F32 = jnp.float32
BF16 = jnp.bfloat16
HIGHEST = lax.Precision.HIGHEST
MESH = pl.DeviceIdType.MESH

FACES = (
    [(0, a, b) for a in range(4) for b in range(4)],
    [(3, a, b) for a in range(4) for b in range(4)],
    [(a, 0, b) for a in range(4) for b in range(4)],
    [(a, 3, b) for a in range(4) for b in range(4)],
    [(a, b, 0) for a in range(4) for b in range(4)],
    [(a, b, 3) for a in range(4) for b in range(4)],
)


def iota(shape, dim):
    return lax.broadcasted_iota(jnp.int32, shape, dim)


def dot(a, b):
    return jnp.dot(a, b, preferred_element_type=F32)


def split_pair(x):
    low = iota(x.shape, 0) < 4
    turned = pltpu.roll(x, 4, 0)
    tiles = []
    for d in (jnp.where(low, x, turned), jnp.where(low, turned, x)):
        rest = d - d.astype(BF16).astype(F32)
        tiles.append(jnp.where(low, d, rest))
    return tiles


def kernel(
    n_space,
    n_slab,
    source,
    initial,
    inverse,
    lift,
    lift_time,
    links,
    orient,
    exports,
    counts,
    out,
    v_source,
    v_initial,
    v_inverse,
    v_lift,
    v_lift_time,
    v_links,
    v_orient,
    v_exports,
    s_counts,
    pick,
    pick_out,
    table,
    gathered,
    nbr,
    lhs_node,
    lhs_time,
    const_node,
    const_time,
    lift_all,
    spread,
    link_rows,
    turn_rows,
    nodes,
    fresh,
    send,
    arrived,
    top_send,
    top_arrived,
    result,
    in_sem,
    send_sem,
    recv_sem,
    top_send_sem,
    top_recv_sem,
    out_sem,
):
    space = lax.axis_index("space")
    slab = lax.axis_index("slab")
    upper = {"space": lax.rem(space + 1, n_space)}
    lower = {"space": lax.rem(space + n_space - 1, n_space)}

    def keep(state):
        fresh[0] = state[:, :128]
        fresh[1] = state[:, 128:]

    loads = []
    for at, (src, dst) in enumerate(
        (
            (exports, v_exports),
            (inverse, v_inverse),
            (source.at[0], v_source),
            (lift_time, v_lift_time),
            (initial, v_initial),
            (links, v_links),
            (orient, v_orient),
            (lift, v_lift),
            (counts, s_counts),
        )
    ):
        copy = pltpu.make_async_copy(src, dst, in_sem.at[at])
        copy.start()
        loads.append(copy)

    barrier = pltpu.get_barrier_semaphore()
    for peer in (lower, upper):
        pl.semaphore_signal(barrier, inc=1, device_id=peer, device_id_type=MESH)

    @pl.when(slab > 0)
    def _():
        pl.semaphore_signal(barrier, inc=1, device_id={"slab": slab - 1}, device_id_type=MESH)

    @pl.when(slab < n_slab - 1)
    def _():
        pl.semaphore_signal(barrier, inc=1, device_id={"slab": slab + 1}, device_id_type=MESH)

    loads[0].wait()
    wanted = jnp.broadcast_to(v_exports[...], (16, E))

    @pl.loop(0, LOCAL // 16)
    def _(step):
        row = pl.multiple_of(step * 16, 16)
        hit = wanted == iota((16, E), 0) + row
        pick_out[pl.ds(row, 16), :] = jnp.where(hit, 1.0, 0.0).astype(BF16)

    loads[3].wait()
    loads[4].wait()
    start = jnp.dot(
        v_lift_time[...], v_initial[...], precision=HIGHEST, preferred_element_type=F32
    )
    loads[1].wait()
    loads[2].wait()
    rhs = v_source[...] + jnp.where(slab == 0, start, 0.0)
    first = jnp.dot(v_inverse[...], rhs, precision=HIGHEST, preferred_element_type=F32)
    const_time[...] = first
    by_node = jnp.where(
        iota((E, E), 1) == (iota((E, E), 0) & 3) * 64 + (iota((E, E), 0) >> 2), 1.0, 0.0
    ).astype(BF16)
    first_high = first.astype(BF16)
    first_low = (first - first_high.astype(F32)).astype(BF16)
    const_node[...] = dot(by_node, first_high) + dot(by_node, first_low)
    keep(const_node[...])

    def space_copies(turn):
        return [
            pltpu.make_async_remote_copy(
                src_ref=send.at[turn, way],
                dst_ref=arrived.at[turn, 1 - way],
                send_sem=send_sem.at[turn, way],
                recv_sem=recv_sem.at[turn, 1 - way],
                device_id=peer,
                device_id_type=MESH,
            )
            for way, peer in ((0, lower), (1, upper))
        ]

    def top_copy(turn):
        return pltpu.make_async_remote_copy(
            src_ref=top_send.at[turn],
            dst_ref=top_arrived.at[turn],
            send_sem=top_send_sem.at[turn],
            recv_sem=top_recv_sem.at[turn],
            device_id={"slab": lax.rem(slab + 1, n_slab)},
            device_id_type=MESH,
        )

    def publish(turn):
        for pair in range(32):
            for half in range(2):
                at = slice(half * 128, half * 128 + 128)
                one, two = split_pair(fresh[half, pair * 8 : pair * 8 + 8, :])
                nodes[2 * pair, :, at] = one
                nodes[2 * pair + 1, :, at] = two
        for face, members in enumerate(FACES):
            for half in range(8):
                rows = [
                    nodes[i * 16 + j * 4 + k] for i, j, k in members[2 * half : 2 * half + 2]
                ]
                table[half * 16 : half * 16 + 16, face * E : face * E + E] = jnp.concatenate(
                    rows, axis=0
                ).astype(BF16)
        leaving = dot(table[:, :LOCAL], pick_out[...])
        low = iota((8, E), 0) < 4
        for half in range(8):
            sums = []
            for at in (2 * half, 2 * half + 1):
                tile = leaving[at * 8 : at * 8 + 8, :]
                sums.append(tile + pltpu.roll(tile, 4, 0))
            rows = jnp.where(low, sums[0], sums[1])
            send[turn, 0, half * 8 : half * 8 + 8, :] = rows[:, :PEER]
            send[turn, 1, half * 8 : half * 8 + 8, :] = rows[:, PEER:]
        for copy in space_copies(turn):
            copy.start()
        for half in range(2):
            top_send[turn, :, half * 128 : half * 128 + 128] = fresh[half, pl.ds(3, 64, stride=4), :]

        @pl.when(slab < n_slab - 1)
        def _():
            top_copy(turn).start()

    def gather_local():
        for face in range(6):
            at = slice(face * E, face * E + E)
            gathered[:, at] = dot(table[:, :LOCAL], pick[:LOCAL, at])

    def advance(turn, lhs, const):
        @pl.when(slab > 0)
        def _():
            top_copy(turn).wait_recv()
            top = top_arrived[turn]
            high = top.astype(BF16)
            nbr[768:832, :] = high
            nbr[832:896, :] = (top - high.astype(F32)).astype(BF16)

        for copy in space_copies(turn):
            copy.wait_recv()
        for way in range(2):
            for half in range(8):
                pair = split_pair(arrived[turn, way, half * 8 : half * 8 + 8, :])
                table[
                    half * 16 : half * 16 + 16, LOCAL + way * PEER : LOCAL + way * PEER + PEER
                ] = jnp.concatenate(pair, axis=0).astype(BF16)
        for face in range(6):
            at = slice(face * E, face * E + E)
            block = gathered[:, at] + dot(table[:, LOCAL:], pick[LOCAL:, at])
            turn_code = turn_rows[face]
            swap = (turn_code & 4) > 0
            back_a = (turn_code & 1) > 0
            back_b = (turn_code & 2) > 0
            v = [[block[(a * 4 + b) * 8 : (a * 4 + b) * 8 + 8, :] for b in range(4)] for a in range(4)]
            v = [[v[a][b] if a == b else jnp.where(swap, v[b][a], v[a][b]) for b in range(4)] for a in range(4)]
            v = [[jnp.where(back_a, v[3 - a][b], v[a][b]) for b in range(4)] for a in range(4)]
            v = [[jnp.where(back_b, v[a][3 - b], v[a][b]) for b in range(4)] for a in range(4)]
            for a in range(4):
                for b in (0, 2):
                    row = face * 128 + (a * 4 + b) * 8
                    nbr[row : row + 16, :] = jnp.concatenate([v[a][b], v[a][b + 1]], axis=0).astype(BF16)
        high = dot(lhs[:E, :], nbr[...])
        low = dot(lhs[E:, :], nbr[...])
        return const[...] + high + low

    count = jnp.where(slab > 0, 1, 0) + jnp.where(slab < n_slab - 1, 1, 0) + 2
    pl.semaphore_wait(barrier, count)
    publish(0)

    loads[5].wait()
    loads[6].wait()
    for face in range(6):
        link_rows[:, face * E : face * E + E] = jnp.broadcast_to(v_links[face : face + 1, :], (16, E))
        turn_rows[face] = jnp.broadcast_to(v_orient[face : face + 1, :], (8, E))

    @pl.loop(0, TABLE // 16)
    def _(step):
        row = pl.multiple_of(step * 16, 16)
        hit = link_rows[...] == iota((16, LOCAL), 0) + row
        pick[pl.ds(row, 16), :] = jnp.where(hit, 1.0, 0.0).astype(BF16)

    column = iota((512, K), 1)
    face_source = ((column & 3) * 16 + ((column >> 3) & 15)) * 6 + (column >> 7)
    wanted_row = jnp.where(column < 768, face_source, 384 + (column & 63))
    spread[...] = jnp.where(iota((512, K), 0) == wanted_row, 1.0, 0.0).astype(BF16)
    loads[7].wait()
    lift_all[:, :384] = v_lift[...]
    lift_all[:, 384:] = jnp.zeros((E, 128), F32)
    lift_all[:, 384:448] = v_lift_time[...]
    operator = jnp.dot(v_inverse[...], lift_all[...], precision=HIGHEST, preferred_element_type=F32)
    high = operator.astype(BF16)
    low = (operator - high.astype(F32)).astype(BF16)
    lhs_time[:E, :] = dot(high, spread[...]).astype(BF16)
    lhs_time[E:, :] = dot(low, spread[...]).astype(BF16)
    lhs_node[:E, :] = dot(by_node, lhs_time[:E, :]).astype(BF16)
    lhs_node[E:, :] = dot(by_node, lhs_time[E:, :]).astype(BF16)
    nbr[768:, :] = jnp.zeros((128, E), BF16)

    @pl.loop(0, ROUNDS - 1)
    def _(turn):
        gather_local()
        keep(advance(turn, lhs_node, const_node))
        publish(turn + 1)

    gather_local()
    last = advance(ROUNDS - 1, lhs_time, const_time)
    loads[8].wait()
    live = iota((E, E), 1) < s_counts[0]
    result[...] = jnp.where(live, last, 0.0)
    copy_out = pltpu.make_async_copy(result, out.at[0], out_sem)
    copy_out.start()

    @pl.loop(0, ROUNDS)
    def _(turn):
        for copy in space_copies(turn):
            copy.wait_send()

        @pl.when(slab < n_slab - 1)
        def _():
            top_copy(turn).wait_send()

    copy_out.wait()


def body(n_space, n_slab, source, initial, inverse, lift, lift_time, links, orient, exports, counts):
    anywhere = pl.BlockSpec(memory_space=pl.ANY)
    vmem = pltpu.VMEM
    dma = pltpu.SemaphoreType.DMA
    return pl.pallas_call(
        functools.partial(kernel, n_space, n_slab),
        name="window",
        out_shape=jax.ShapeDtypeStruct((1, 256, E), F32),
        in_specs=[anywhere] * 9,
        out_specs=anywhere,
        scratch_shapes=[
            vmem((256, E), F32),
            vmem((64, E), F32),
            vmem((256, 256), F32),
            vmem((256, 384), F32),
            vmem((256, 64), F32),
            vmem((6, E), jnp.int32),
            vmem((6, E), jnp.int32),
            vmem((1, E), jnp.int32),
            pltpu.SMEM((1,), jnp.int32),
            vmem((TABLE, LOCAL), BF16),
            vmem((LOCAL, 2 * PEER), BF16),
            vmem((128, TABLE), BF16),
            vmem((128, LOCAL), F32),
            vmem((K, E), BF16),
            vmem((512, K), BF16),
            vmem((512, K), BF16),
            vmem((256, E), F32),
            vmem((256, E), F32),
            vmem((256, 512), F32),
            vmem((512, K), BF16),
            vmem((16, LOCAL), jnp.int32),
            vmem((6, 8, E), jnp.int32),
            vmem((64, 8, E), F32),
            vmem((2, 256, 128), F32),
            vmem((ROUNDS, 2, 64, PEER), F32),
            vmem((ROUNDS, 2, 64, PEER), F32),
            vmem((ROUNDS, 64, E), F32),
            vmem((ROUNDS, 64, E), F32),
            vmem((256, E), F32),
            dma((9,)),
            dma((ROUNDS, 2)),
            dma((ROUNDS, 2)),
            dma((ROUNDS,)),
            dma((ROUNDS,)),
            dma,
        ],
        compiler_params=pltpu.CompilerParams(
            collective_id=0, has_side_effects=True, vmem_limit_bytes=48 * 1024 * 1024
        ),
    )(source, initial, inverse, lift, lift_time, links, orient, exports.reshape(1, E), counts)


def solution(mesh):
    return jax.shard_map(
        functools.partial(body, mesh.shape["space"], mesh.shape["slab"]),
        mesh=mesh,
        in_specs=(
            P("slab", None, "space"),
            P(None, "space"),
            P(),
            P(),
            P(),
            P(None, "space"),
            P(None, "space"),
            P("space"),
            P("space"),
        ),
        out_specs=P("slab", None, "space"),
        check_vma=False,
    )
```

time: 98.4 us -> 40.8 us (0.41)
  the two profiles are of different devices: /device:TPU:121 before, /device:TPU:6 now
where the time goes in v1:
time: 40.8 us; the launch traced here: 40.5 us
  Pallas kernels  35.2 us (86%)
  local copies, waits for them, and re-layouts  4.58 us (11%)
  between operations  0.74 us (2%)
    pallas_call x1, Pallas kernels, body(): pl.pallas_call(functools.partial(kernel, n_space, n_slab), name='window',...  35.2 us
    unnamed x16, local copies, waits for them, and re-layouts  4.58 us

profile of v1, /device:TPU:6, one launch (start us, length us, event | category | flops | bytes accessed | tf_op | source)
XLA Modules:
  0.0 40.5 jit_solution(17620426787914104193)
XLA Ops:
  0.7 0.0 copy-start.3
  0.7 0.0 copy-start.4
  0.7 0.0 copy-start.5
  0.7 0.0 copy-start.6
  0.7 1.0 %copy.10.lift_time = f32[256,64]{1,0:T(8,128)S(1)} copy(f32[256,64]{0,1:T(8,128)} %param.13) | data formatting | bytes 131072 | tf_op args[4]
  1.7 0.0 copy-done.3
  1.7 0.0 copy-done.4
  1.7 0.0 copy-done.5
  1.7 0.0 copy-done.6
  1.7 0.0 copy-start
  1.7 1.0 %copy-done = f32[256,384]{1,0:T(8,128)S(1)} copy-done((f32[256,384]{1,0:T(8,128)S(1)}, f32[256,384]{1,0:T(8,128)}, u32[]{:S(2)}) %copy-start) | copy-done | bytes 393240
  2.7 0.0 copy-start.1
  2.7 0.9 %copy-done.1 = f32[1,256,256]{2,1,0:T(8,128)S(1)} copy-done((f32[1,256,256]{2,1,0:T(8,128)S(1)}, f32[1,256,256]{2,1,0:T(8,128)}, u32[]{:S(2)}) %copy-start.1) | copy-done | bytes 262168
  3.7 0.0 copy-start.2
  3.7 0.9 %copy-done.2 = f32[256,256]{1,0:T(8,128)S(1)} copy-done((f32[256,256]{1,0:T(8,128)S(1)}, f32[256,256]{1,0:T(8,128)}, u32[]{:S(2)}) %copy-start.2) | copy-done | bytes 262168
  4.6 35.2 %window.1 = f32[1,256,256]{2,1,0:T(8,128)S(1)} custom-call(f32[1,256,256]{2,1,0:T(8,128)S(1)} %copy-done.1, f32[64,256]{1,0:T(8,128)S(1)} %copy-done.3, f32[256,256]{1,0:T(8,128)S(1)} %copy-done.2, f32[256,384]{1,0:T(8,128)S(1)} %copy-done, f32[256,64]{1,0:T(8,128)S(1)} %copy.10.lift_time, s32[6,256]{1,0:T(8,128)S(1)} %copy-done.4, s32[6,256]{1,0:T(8,128)S(1)} %copy-done.5, ...), custom_call_target="tpu_custom_call" | custom-call | tf_op jit(solution)/shard_map/window/pallas_call | solution.py:325
  39.8 0.7 %copy.13 = f32[1,256,256]{2,1,0:T(8,128)} copy(f32[1,256,256]{2,1,0:T(8,128)S(1)} %window.1) | data formatting | bytes 524288
Async XLA Ops:
  0.7 1.0 %copy-start.3 = (f32[64,256]{1,0:T(8,128)S(1)}, f32[64,256]{1,0:T(8,128)}, u32[]{:S(2)}) copy-start(f32[64,256]{1,0:T(8,128)} %initial.1) | copy-start | bytes 196612
  0.7 1.0 %copy-start.4 = (s32[6,256]{1,0:T(8,128)S(1)}, s32[6,256]{1,0:T(8,128)}, u32[]{:S(2)}) copy-start(s32[6,256]{1,0:T(8,128)} %links.1) | copy-start | bytes 18436
  0.7 1.0 %copy-start.5 = (s32[6,256]{1,0:T(8,128)S(1)}, s32[6,256]{1,0:T(8,128)}, u32[]{:S(2)}) copy-start(s32[6,256]{1,0:T(8,128)} %orient.1) | copy-start | bytes 18436
  0.7 1.0 %copy-start.6 = (s32[256]{0:T(256)S(1)}, s32[256]{0:T(256)}, u32[]{:S(2)}) copy-start(s32[256]{0:T(256)} %param.16) | copy-start | bytes 3076
  1.7 1.0 %copy-start = (f32[256,384]{1,0:T(8,128)S(1)}, f32[256,384]{1,0:T(8,128)}, u32[]{:S(2)}) copy-start(f32[256,384]{1,0:T(8,128)} %lift.1) | copy-start | bytes 1179652
  2.7 0.9 %copy-start.1 = (f32[1,256,256]{2,1,0:T(8,128)S(1)}, f32[1,256,256]{2,1,0:T(8,128)}, u32[]{:S(2)}) copy-start(f32[1,256,256]{2,1,0:T(8,128)} %source.1) | copy-start | bytes 786436
  3.7 0.9 %copy-start.2 = (f32[256,256]{1,0:T(8,128)S(1)}, f32[256,256]{1,0:T(8,128)}, u32[]{:S(2)}) copy-start(f32[256,256]{1,0:T(8,128)} %inverse.1) | copy-start | bytes 786436

commit v2 on v1

--- a/solution.py
+++ b/solution.py
@@ -57,7 +57,6 @@
     links,
     orient,
     exports,
-    counts,
     out,
     v_source,
     v_initial,
@@ -67,7 +66,6 @@
     v_links,
     v_orient,
     v_exports,
-    s_counts,
     pick,
     pick_out,
     table,
@@ -87,13 +85,11 @@
     arrived,
     top_send,
     top_arrived,
-    result,
     in_sem,
     send_sem,
     recv_sem,
     top_send_sem,
     top_recv_sem,
-    out_sem,
 ):
     space = lax.axis_index("space")
     slab = lax.axis_index("slab")
@@ -115,7 +111,6 @@
             (links, v_links),
             (orient, v_orient),
             (lift, v_lift),
-            (counts, s_counts),
         )
     ):
         copy = pltpu.make_async_copy(src, dst, in_sem.at[at])
@@ -146,7 +141,7 @@
     loads[3].wait()
     loads[4].wait()
     start = jnp.dot(
-        v_lift_time[...], v_initial[...], precision=HIGHEST, preferred_element_type=F32
+        v_lift_time[...].T, v_initial[...], precision=HIGHEST, preferred_element_type=F32
     )
     loads[1].wait()
     loads[2].wait()
@@ -282,7 +277,7 @@
     loads[7].wait()
     lift_all[:, :384] = v_lift[...]
     lift_all[:, 384:] = jnp.zeros((E, 128), F32)
-    lift_all[:, 384:448] = v_lift_time[...]
+    lift_all[:, 384:448] = v_lift_time[...].T
     operator = jnp.dot(v_inverse[...], lift_all[...], precision=HIGHEST, preferred_element_type=F32)
     high = operator.astype(BF16)
     low = (operator - high.astype(F32)).astype(BF16)
@@ -300,11 +295,7 @@
 
     gather_local()
     last = advance(ROUNDS - 1, lhs_time, const_time)
-    loads[8].wait()
-    live = iota((E, E), 1) < s_counts[0]
-    result[...] = jnp.where(live, last, 0.0)
-    copy_out = pltpu.make_async_copy(result, out.at[0], out_sem)
-    copy_out.start()
+    out[0] = last
 
     @pl.loop(0, ROUNDS)
     def _(turn):
@@ -315,29 +306,28 @@
         def _():
             top_copy(turn).wait_send()
 
-    copy_out.wait()
-
 
 def body(n_space, n_slab, source, initial, inverse, lift, lift_time, links, orient, exports, counts):
-    anywhere = pl.BlockSpec(memory_space=pl.ANY)
+    hbm = pl.BlockSpec(memory_space=pltpu.HBM)
+    arrays = (source, initial, inverse, lift, lift_time.T, links, orient, exports.reshape(1, E))
+    arrays = [pltpu.with_memory_space_constraint(array, pltpu.HBM) for array in arrays]
     vmem = pltpu.VMEM
     dma = pltpu.SemaphoreType.DMA
-    return pl.pallas_call(
+    state = pl.pallas_call(
         functools.partial(kernel, n_space, n_slab),
         name="window",
         out_shape=jax.ShapeDtypeStruct((1, 256, E), F32),
-        in_specs=[anywhere] * 9,
-        out_specs=anywhere,
+        in_specs=[hbm] * 8,
+        out_specs=pl.BlockSpec(memory_space=pltpu.VMEM),
         scratch_shapes=[
             vmem((256, E), F32),
             vmem((64, E), F32),
             vmem((256, 256), F32),
             vmem((256, 384), F32),
-            vmem((256, 64), F32),
+            vmem((64, 256), F32),
             vmem((6, E), jnp.int32),
             vmem((6, E), jnp.int32),
             vmem((1, E), jnp.int32),
-            pltpu.SMEM((1,), jnp.int32),
             vmem((TABLE, LOCAL), BF16),
             vmem((LOCAL, 2 * PEER), BF16),
             vmem((128, TABLE), BF16),
@@ -357,18 +347,18 @@
             vmem((ROUNDS, 2, 64, PEER), F32),
             vmem((ROUNDS, 64, E), F32),
             vmem((ROUNDS, 64, E), F32),
-            vmem((256, E), F32),
-            dma((9,)),
+            dma((8,)),
             dma((ROUNDS, 2)),
             dma((ROUNDS, 2)),
             dma((ROUNDS,)),
             dma((ROUNDS,)),
-            dma,
         ],
         compiler_params=pltpu.CompilerParams(
             collective_id=0, has_side_effects=True, vmem_limit_bytes=48 * 1024 * 1024
         ),
-    )(source, initial, inverse, lift, lift_time, links, orient, exports.reshape(1, E), counts)
+    )(*arrays)
+    live = jnp.arange(E, dtype=jnp.int32) < counts[0]
+    return jnp.where(live[None, None, :], state, 0.0)
 
 
 def solution(mesh):

time: 40.8 us -> 36.6 us (0.90)
  local copies, waits for them, and re-layouts: 4.58 us -> 0 us
  other arithmetic: 0 us -> 0.73 us
    unnamed x16 -> x0, local copies, waits for them, and re-layouts: 4.58 us -> none
    select_n x0 -> x1, other arithmetic: none -> 0.72 us  [body(): return jnp.where(live[None, None, :], state, 0.0)]
where the time goes in v2:
time: 36.6 us; the launch traced here: 36.5 us
  Pallas kernels  35.1 us (96%)
  other arithmetic  0.73 us (2%)
  between operations  0.67 us (2%)
    pallas_call x1, Pallas kernels, body(): pl.pallas_call(functools.partial(kernel, n_space, n_slab), name='window',...  35.1 us

profile of v2, /device:TPU:6, one launch (start us, length us, event | category | flops | bytes accessed | tf_op | source)
XLA Modules:
  0.0 36.5 jit_solution(5930044538820304171)
XLA Ops:
  0.7 35.1 %window.1 = f32[1,256,256]{2,1,0:T(8,128)S(1)} custom-call(f32[1,256,256]{2,1,0:T(8,128)} %source.1, f32[64,256]{1,0:T(8,128)} %initial.1, f32[256,256]{1,0:T(8,128)} %inverse.1, f32[256,384]{1,0:T(8,128)} %lift.1, f32[64,256]{1,0:T(8,128)} %bitcast.4, s32[6,256]{1,0:T(8,128)} %links.1, s32[6,256]{1,0:T(8,128)} %orient.1, s32[1,256]{1,0:T(1,128)} %bitcast.5), custom_call_target="tpu_custom_call" | custom-call | tf_op jit(solution)/shard_map/window/pallas_call | solution.py:316
  35.8 0.7 %broadcast_select_fusion = f32[1,256,256]{2,1,0:T(8,128)} fusion(f32[1,256,256]{2,1,0:T(8,128)S(1)} %window.1, pred[256]{0:T(512)(128)(4,1)S(1)} %iota_compare_fusion), kind=kLoop, calls=%fused_computation | loop fusion | flops 65536 | bytes 524544 | tf_op jit(solution)/shard_map/jit(_where)/select_n | solution.py:361
  (1 shorter events, 0.0 us)

commit v3 on v2

v3 whole, which is shorter than its diff:
```python
import functools

import jax
import jax.numpy as jnp
from jax import lax
from jax.experimental import pallas as pl
from jax.experimental.pallas import tpu as pltpu
from jax.sharding import PartitionSpec as P

ROUNDS = 5
E = 256
PEER = 128
LOCAL = 6 * E
TABLE = LOCAL + 2 * PEER
NBR = 6 * 128
K = NBR + 128
F32 = jnp.float32
BF16 = jnp.bfloat16
HIGHEST = lax.Precision.HIGHEST
MESH = pl.DeviceIdType.MESH

FACES = (
    [(0, a, b) for a in range(4) for b in range(4)],
    [(3, a, b) for a in range(4) for b in range(4)],
    [(a, 0, b) for a in range(4) for b in range(4)],
    [(a, 3, b) for a in range(4) for b in range(4)],
    [(a, b, 0) for a in range(4) for b in range(4)],
    [(a, b, 3) for a in range(4) for b in range(4)],
)


def iota(shape, dim):
    return lax.broadcasted_iota(jnp.int32, shape, dim)


def dot(a, b):
    return jnp.dot(a, b, preferred_element_type=F32)


def halves(x):
    high = x.astype(BF16)
    return high, (x - high.astype(F32)).astype(BF16)


def split_pair(x):
    low = iota(x.shape, 0) < 4
    turned = pltpu.roll(x, 4, 0)
    tiles = []
    for d in (jnp.where(low, x, turned), jnp.where(low, turned, x)):
        rest = d - d.astype(BF16).astype(F32)
        tiles.append(jnp.where(low, d, rest))
    return tiles


def oriented(block, code):
    swap = (code & 4) > 0
    back_a = (code & 1) > 0
    back_b = (code & 2) > 0
    four = range(4)
    v = [[block[(a * 4 + b) * 8 : (a * 4 + b) * 8 + 8, :] for b in four] for a in four]
    v = [[v[a][b] if a == b else jnp.where(swap, v[b][a], v[a][b]) for b in four] for a in four]
    v = [[jnp.where(back_a, v[3 - a][b], v[a][b]) for b in four] for a in four]
    v = [[jnp.where(back_b, v[a][3 - b], v[a][b]) for b in four] for a in four]
    return [v[a][b] for a in four for b in four]


def face_traces(state, code):
    low = iota(code.shape, 0) < 4

    def tile(node):
        return state[node * 4 : node * 4 + 8, :]

    rows = []
    for half in range(8):
        a, b = half // 2, 2 * (half % 2)
        near, far = a * 16 + b * 4, a * 16 + b * 4 + 4
        choices = [
            tile(a * 4 + b),
            tile(48 + a * 4 + b),
            tile(a * 16 + b),
            tile(a * 16 + 12 + b),
            jnp.where(low, tile(near), pltpu.roll(tile(far), 4, 0)),
            jnp.where(low, pltpu.roll(tile(near + 2), 4, 0), tile(far + 2)),
        ]
        value = choices[0]
        for face in range(1, 6):
            value = jnp.where(code == face, choices[face], value)
        rows.append(value)
    return rows


def kernel(
    n_space,
    n_slab,
    source,
    initial,
    inverse,
    lift,
    lift_time,
    links,
    orient,
    exports,
    out,
    v_source,
    v_initial,
    v_inverse,
    v_lift,
    v_lift_time,
    v_links,
    v_orient,
    v_exports,
    pick,
    pick_near,
    table,
    nbr,
    nbr_far,
    lhs_node,
    lhs_time,
    inv_node,
    const_node,
    own,
    own_out,
    lift_all,
    spread,
    link_rows,
    turn_rows,
    turn_out,
    codes,
    select,
    nodes,
    fresh,
    send,
    arrived,
    top_send,
    top_arrived,
    in_sem,
    send_sem,
    recv_sem,
    top_send_sem,
    top_recv_sem,
):
    space = lax.axis_index("space")
    slab = lax.axis_index("slab")
    upper = {"space": lax.rem(space + 1, n_space)}
    lower = {"space": lax.rem(space + n_space - 1, n_space)}

    loads = []
    for at, (src, dst) in enumerate(
        (
            (exports, v_exports),
            (lift_time, v_lift_time),
            (initial, v_initial),
            (inverse, v_inverse),
            (source.at[0], v_source),
            (links, v_links),
            (orient, v_orient),
            (lift, v_lift),
        )
    ):
        copy = pltpu.make_async_copy(src, dst, in_sem.at[at])
        copy.start()
        loads.append(copy)

    barrier = pltpu.get_barrier_semaphore()
    for peer in (lower, upper):
        pl.semaphore_signal(barrier, inc=1, device_id=peer, device_id_type=MESH)

    @pl.when(slab > 0)
    def _():
        pl.semaphore_signal(barrier, inc=1, device_id={"slab": slab - 1}, device_id_type=MESH)

    @pl.when(slab < n_slab - 1)
    def _():
        pl.semaphore_signal(barrier, inc=1, device_id={"slab": slab + 1}, device_id_type=MESH)

    def space_copies(turn):
        return [
            pltpu.make_async_remote_copy(
                src_ref=send.at[turn, way],
                dst_ref=arrived.at[turn, 1 - way],
                send_sem=send_sem.at[turn, way],
                recv_sem=recv_sem.at[turn, 1 - way],
                device_id=peer,
                device_id_type=MESH,
            )
            for way, peer in ((0, lower), (1, upper))
        ]

    def top_copy(turn):
        return pltpu.make_async_remote_copy(
            src_ref=top_send.at[turn],
            dst_ref=top_arrived.at[turn],
            send_sem=top_send_sem.at[turn],
            recv_sem=top_recv_sem.at[turn],
            device_id={"slab": lax.rem(slab + 1, n_slab)},
            device_id_type=MESH,
        )

    def send_out(turn, state):
        code = jnp.broadcast_to(v_exports[...] >> 8, (8, E))
        for half, rows in enumerate(face_traces(state, code)):
            send[turn, 0, half * 8 : half * 8 + 8, :] = rows[:, :PEER]
            send[turn, 1, half * 8 : half * 8 + 8, :] = rows[:, PEER:]
        for copy in space_copies(turn):
            copy.start()

    def keep(turn, state):
        for half in range(2):
            fresh[half] = state[:, half * 128 : half * 128 + 128]
        for half in range(2):
            top_send[turn, :, half * 128 : half * 128 + 128] = fresh[half, pl.ds(3, 64, stride=4), :]

        @pl.when(slab < n_slab - 1)
        def _():
            top_copy(turn).start()

    def exported(state):
        high, low = halves(state)
        return dot(high, select[...]) + dot(low, select[...])

    loads[0].wait()
    element = jnp.broadcast_to(v_exports[...] & 255, (E, E))
    select[...] = jnp.where(element == iota((E, E), 0), 1.0, 0.0).astype(BF16)
    by_node = jnp.where(
        iota((E, E), 1) == (iota((E, E), 0) & 3) * 64 + (iota((E, E), 0) >> 2), 1.0, 0.0
    ).astype(BF16)
    loads[1].wait()
    loads[2].wait()
    time_high, time_low = halves(v_lift_time[...].T)
    first_high, first_low = halves(v_initial[...])
    start = dot(time_high, first_high) + dot(time_high, first_low) + dot(time_low, first_high)
    loads[3].wait()
    inv_high, inv_low = halves(v_inverse[...])
    inv_node[:E, :] = dot(by_node, inv_high).astype(BF16)
    inv_node[E:, :] = dot(by_node, inv_low).astype(BF16)
    loads[4].wait()
    rhs_high, rhs_low = halves(v_source[...] + jnp.where(slab == 0, start, 0.0))
    first = dot(inv_node[:E, :], rhs_high) + dot(inv_node[:E, :], rhs_low) + dot(inv_node[E:, :], rhs_high)
    const_node[...] = first
    leaving = exported(first)
    count = jnp.where(slab > 0, 1, 0) + jnp.where(slab < n_slab - 1, 1, 0) + 2
    pl.semaphore_wait(barrier, count)
    send_out(0, leaving)
    keep(0, first)

    loads[5].wait()
    loads[6].wait()
    codes[...] = jnp.zeros((32, E), F32)
    codes[0:6, :] = (v_links[...] >> 8).astype(F32)
    codes[8:14, :] = (v_links[...] & 255).astype(F32)
    codes[16:22, :] = v_orient[...].astype(F32)
    moved = dot(codes[...].astype(BF16), select[...])
    far_link = (moved[0:8, :] * 256.0 + moved[8:16, :]).astype(jnp.int32)
    far_turn = moved[16:24, :].astype(jnp.int32)
    for face in range(6):
        at = slice(face * E, face * E + E)
        link_rows[:, at] = jnp.broadcast_to(v_links[face : face + 1, :], (16, E))
        turn_rows[face] = jnp.broadcast_to(v_orient[face : face + 1, :], (8, E))
        turn_out[face] = jnp.broadcast_to(far_turn[face : face + 1, :], (8, E))
        wanted = jnp.broadcast_to(far_link[face : face + 1, :], (2 * PEER, E))
        pick_near[:, at] = jnp.where(wanted == iota((2 * PEER, E), 0) + LOCAL, 1.0, 0.0).astype(BF16)

    @pl.loop(0, TABLE // 16)
    def _(step):
        row = pl.multiple_of(step * 16, 16)
        hit = link_rows[...] == iota((16, LOCAL), 0) + row
        pick[pl.ds(row, 16), :] = jnp.where(hit, 1.0, 0.0).astype(BF16)

    column = iota((512, K), 1)
    face_source = ((column & 3) * 16 + ((column >> 3) & 15)) * 6 + (column >> 7)
    wanted_row = jnp.where(column < NBR, face_source, 384 + (column & 63))
    spread[...] = jnp.where(iota((512, K), 0) == wanted_row, 1.0, 0.0).astype(BF16)
    loads[7].wait()
    lift_all[:, :384] = v_lift[...]
    lift_all[:, 384:] = jnp.zeros((E, 128), F32)
    lift_all[:, 384:448] = v_lift_time[...].T
    lift_high, lift_low = halves(lift_all[...])
    lhs_time[:E, :] = dot(lift_high, spread[...]).astype(BF16)
    lhs_time[E:, :] = dot(lift_low, spread[...]).astype(BF16)

    def operator(high, low):
        return halves(dot(high, lhs_time[:E, :]) + dot(high, lhs_time[E:, :]) + dot(low, lhs_time[:E, :]))

    node_high, node_low = operator(inv_node[:E, :], inv_node[E:, :])
    lhs_node[:E, :] = node_high
    lhs_node[E:, :] = node_low
    nbr[NBR:, :] = jnp.zeros((128, E), BF16)

    def local_part(turn):
        for pair in range(32):
            for half in range(2):
                at = slice(half * 128, half * 128 + 128)
                one, two = split_pair(fresh[half, pair * 8 : pair * 8 + 8, :])
                nodes[2 * pair, :, at] = one
                nodes[2 * pair + 1, :, at] = two
        for face, members in enumerate(FACES):
            for half in range(8):
                rows = [nodes[i * 16 + j * 4 + k] for i, j, k in members[2 * half : 2 * half + 2]]
                table[half * 16 : half * 16 + 16, face * E : face * E + E] = jnp.concatenate(
                    rows, axis=0
                ).astype(BF16)
        for face in range(6):
            at = slice(face * E, face * E + E)
            store_rows(nbr, face, oriented(dot(table[:, :LOCAL], pick[:LOCAL, at]), turn_rows[face]))

        @pl.when(slab > 0)
        def _():
            top_copy(turn).wait_recv()
            high, low = halves(top_arrived[turn])
            nbr[NBR : NBR + 64, :] = high
            nbr[NBR + 64 :, :] = low

    def store_rows(ref, face, tiles):
        for half in range(8):
            row = face * 128 + half * 16
            ref[row : row + 16, :] = jnp.concatenate(tiles[2 * half : 2 * half + 2], axis=0).astype(BF16)

    def receive(turn):
        for copy in space_copies(turn):
            copy.wait_recv()
        for way in range(2):
            for half in range(8):
                pair = split_pair(arrived[turn, way, half * 8 : half * 8 + 8, :])
                table[
                    half * 16 : half * 16 + 16, LOCAL + way * PEER : LOCAL + way * PEER + PEER
                ] = jnp.concatenate(pair, axis=0).astype(BF16)

    def remote_part(lhs, chosen, base, turns):
        for face in range(6):
            at = slice(face * E, face * E + E)
            block = dot(table[:, LOCAL:], chosen[base : base + 2 * PEER, at])
            store_rows(nbr_far, face, oriented(block, turns[face]))
        return dot(lhs[:E, :NBR], nbr_far[...]) + dot(lhs[E:, :NBR], nbr_far[...])

    @pl.loop(0, ROUNDS - 1)
    def _(turn):
        local_part(turn)
        so_far = const_node[...] + dot(lhs_node[:E, :], nbr[...]) + dot(lhs_node[E:, :], nbr[...])
        own[...] = so_far
        own_out[...] = exported(so_far)
        receive(turn)
        send_out(turn + 1, own_out[...] + remote_part(lhs_node, pick_near, 0, turn_out))
        keep(turn + 1, own[...] + remote_part(lhs_node, pick, LOCAL, turn_rows))

    inv_high, inv_low = halves(v_inverse[...])
    rhs_high, rhs_low = halves(v_source[...] + jnp.where(slab == 0, start, 0.0))
    own[...] = dot(inv_high, rhs_high) + dot(inv_high, rhs_low) + dot(inv_low, rhs_high)
    time_high, time_low = operator(inv_high, inv_low)
    lhs_time[:E, :] = time_high
    lhs_time[E:, :] = time_low
    local_part(ROUNDS - 1)
    own[...] += dot(lhs_time[:E, :], nbr[...]) + dot(lhs_time[E:, :], nbr[...])
    receive(ROUNDS - 1)
    out[0] = own[...] + remote_part(lhs_time, pick, LOCAL, turn_rows)

    @pl.loop(0, ROUNDS)
    def _(turn):
        for copy in space_copies(turn):
            copy.wait_send()

        @pl.when(slab < n_slab - 1)
        def _():
            top_copy(turn).wait_send()


def body(n_space, n_slab, source, initial, inverse, lift, lift_time, links, orient, exports, counts):
    hbm = pl.BlockSpec(memory_space=pltpu.HBM)
    arrays = (source, initial, inverse, lift, lift_time.T, links, orient, exports.reshape(1, E))
    arrays = [pltpu.with_memory_space_constraint(array, pltpu.HBM) for array in arrays]
    vmem = pltpu.VMEM
    dma = pltpu.SemaphoreType.DMA
    state = pl.pallas_call(
        functools.partial(kernel, n_space, n_slab),
        name="window",
        out_shape=jax.ShapeDtypeStruct((1, 256, E), F32),
        in_specs=[hbm] * 8,
        out_specs=pl.BlockSpec(memory_space=pltpu.VMEM),
        scratch_shapes=[
            vmem((256, E), F32),
            vmem((64, E), F32),
            vmem((256, 256), F32),
            vmem((256, 384), F32),
            vmem((64, 256), F32),
            vmem((6, E), jnp.int32),
            vmem((6, E), jnp.int32),
            vmem((1, E), jnp.int32),
            vmem((TABLE, LOCAL), BF16),
            vmem((2 * PEER, LOCAL), BF16),
            vmem((128, TABLE), BF16),
            vmem((K, E), BF16),
            vmem((NBR, E), BF16),
            vmem((512, K), BF16),
            vmem((512, K), BF16),
            vmem((512, 256), BF16),
            vmem((256, E), F32),
            vmem((256, E), F32),
            vmem((256, E), F32),
            vmem((256, 512), F32),
            vmem((512, K), BF16),
            vmem((16, LOCAL), jnp.int32),
            vmem((6, 8, E), jnp.int32),
            vmem((6, 8, E), jnp.int32),
            vmem((32, E), F32),
            vmem((E, E), BF16),
            vmem((64, 8, E), F32),
            vmem((2, 256, 128), F32),
            vmem((ROUNDS, 2, 64, PEER), F32),
            vmem((ROUNDS, 2, 64, PEER), F32),
            vmem((ROUNDS, 64, E), F32),
            vmem((ROUNDS, 64, E), F32),
            dma((8,)),
            dma((ROUNDS, 2)),
            dma((ROUNDS, 2)),
            dma((ROUNDS,)),
            dma((ROUNDS,)),
        ],
        compiler_params=pltpu.CompilerParams(
            collective_id=0, has_side_effects=True, vmem_limit_bytes=48 * 1024 * 1024
        ),
    )(*arrays)
    live = jnp.arange(E, dtype=jnp.int32) < counts[0]
    return jnp.where(live[None, None, :], state, 0.0)


def solution(mesh):
    return jax.shard_map(
        functools.partial(body, mesh.shape["space"], mesh.shape["slab"]),
        mesh=mesh,
        in_specs=(
            P("slab", None, "space"),
            P(None, "space"),
            P(),
            P(),
            P(),
            P(None, "space"),
            P(None, "space"),
            P("space"),
            P("space"),
        ),
        out_specs=P("slab", None, "space"),
        check_vma=False,
    )
```

time: 36.6 us -> 35.1 us (0.959)
  Pallas kernels: 35.1 us -> 33.6 us
    pallas_call x1, Pallas kernels: 35.1 us -> 33.6 us  [body(): pl.pallas_call(functools.partial(kernel, n_space, n_slab), name='window',...]
where the time goes in v3:
time: 35.1 us; the launch traced here: 35 us
  Pallas kernels  33.6 us (96%)
  other arithmetic  0.73 us (2%)
  between operations  0.67 us (2%)
    pallas_call x1, Pallas kernels, body(): pl.pallas_call(functools.partial(kernel, n_space, n_slab), name='window',...  33.6 us
    select_n x1, other arithmetic, body(): return jnp.where(live[None, None, :], state, 0.0)  0.72 us

profile of v3, /device:TPU:6, one launch (start us, length us, event | category | flops | bytes accessed | tf_op | source)
XLA Modules:
  0.0 35.0 jit_solution(5026083258316828370)
XLA Ops:
  0.7 33.6 %window.1 = f32[1,256,256]{2,1,0:T(8,128)S(1)} custom-call(f32[1,256,256]{2,1,0:T(8,128)} %source.1, f32[64,256]{1,0:T(8,128)} %initial.1, f32[256,256]{1,0:T(8,128)} %inverse.1, f32[256,384]{1,0:T(8,128)} %lift.1, f32[64,256]{1,0:T(8,128)} %bitcast.4, s32[6,256]{1,0:T(8,128)} %links.1, s32[6,256]{1,0:T(8,128)} %orient.1, s32[1,256]{1,0:T(1,128)} %bitcast.5), custom_call_target="tpu_custom_call" | custom-call | tf_op jit(solution)/shard_map/window/pallas_call | solution.py:372
  34.3 0.7 %broadcast_select_fusion = f32[1,256,256]{2,1,0:T(8,128)} fusion(f32[1,256,256]{2,1,0:T(8,128)S(1)} %window.1, pred[256]{0:T(512)(128)(4,1)S(1)} %iota_compare_fusion), kind=kLoop, calls=%fused_computation | loop fusion | flops 65536 | bytes 524544 | tf_op jit(solution)/shard_map/jit(_where)/select_n | solution.py:422
  (1 shorter events, 0.0 us)

commit v4 on v3

--- a/solution.py
+++ b/solution.py
@@ -50,6 +50,15 @@
         rest = d - d.astype(BF16).astype(F32)
         tiles.append(jnp.where(low, d, rest))
     return tiles
+
+
+def apply(lhs, rows, depth):
+    parts = []
+    for at in (0, 128):
+        parts.append(
+            dot(lhs[at : at + 128, :depth], rows[...]) + dot(lhs[E + at : E + at + 128, :depth], rows[...])
+        )
+    return jnp.concatenate(parts, axis=0)
 
 
 def oriented(block, code):
@@ -133,16 +142,27 @@
     arrived,
     top_send,
     top_arrived,
+    far_send,
+    far_arrived,
+    skip_arrived,
+    far_pick,
+    far_table,
+    far_turn,
+    extra,
     in_sem,
     send_sem,
     recv_sem,
     top_send_sem,
     top_recv_sem,
+    far_sem,
+    skip_sem,
 ):
     space = lax.axis_index("space")
     slab = lax.axis_index("slab")
     upper = {"space": lax.rem(space + 1, n_space)}
     lower = {"space": lax.rem(space + n_space - 1, n_space)}
+    second_upper = {"space": lax.rem(space + 2, n_space)}
+    second_lower = {"space": lax.rem(space + n_space - 2, n_space)}
 
     loads = []
     for at, (src, dst) in enumerate(
@@ -162,7 +182,7 @@
         loads.append(copy)
 
     barrier = pltpu.get_barrier_semaphore()
-    for peer in (lower, upper):
+    for peer in (lower, upper, second_lower, second_upper):
         pl.semaphore_signal(barrier, inc=1, device_id=peer, device_id_type=MESH)
 
     @pl.when(slab > 0)
@@ -178,7 +198,7 @@
             pltpu.make_async_remote_copy(
                 src_ref=send.at[turn, way],
                 dst_ref=arrived.at[turn, 1 - way],
-                send_sem=send_sem.at[turn, way],
+                send_sem=send_sem.at[way],
                 recv_sem=recv_sem.at[turn, 1 - way],
                 device_id=peer,
                 device_id_type=MESH,
@@ -186,25 +206,44 @@
             for way, peer in ((0, lower), (1, upper))
         ]
 
+    def other_copies(source_of, target, sems, peers):
+        return [
+            pltpu.make_async_remote_copy(
+                src_ref=source_of(way),
+                dst_ref=target.at[1 - way],
+                send_sem=sems.at[0, way],
+                recv_sem=sems.at[1, 1 - way],
+                device_id=peer,
+                device_id_type=MESH,
+            )
+            for way, peer in enumerate(peers)
+        ]
+
+    far_copies = other_copies(lambda way: far_send.at[way], far_arrived, far_sem, (lower, upper))
+    skip_copies = other_copies(lambda way: send.at[0, way], skip_arrived, skip_sem, (second_lower, second_upper))
+
     def top_copy(turn):
         return pltpu.make_async_remote_copy(
             src_ref=top_send.at[turn],
             dst_ref=top_arrived.at[turn],
-            send_sem=top_send_sem.at[turn],
+            send_sem=top_send_sem,
             recv_sem=top_recv_sem.at[turn],
             device_id={"slab": lax.rem(slab + 1, n_slab)},
             device_id_type=MESH,
         )
 
-    def send_out(turn, state):
+    def send_out(turn, state, turn_is_later=True):
         code = jnp.broadcast_to(v_exports[...] >> 8, (8, E))
         for half, rows in enumerate(face_traces(state, code)):
             send[turn, 0, half * 8 : half * 8 + 8, :] = rows[:, :PEER]
             send[turn, 1, half * 8 : half * 8 + 8, :] = rows[:, PEER:]
+        if turn_is_later:
+            for copy in space_copies(turn - 1):
+                copy.wait_send()
         for copy in space_copies(turn):
             copy.start()
 
-    def keep(turn, state):
+    def keep(turn, state, turn_is_later=True):
         for half in range(2):
             fresh[half] = state[:, half * 128 : half * 128 + 128]
         for half in range(2):
@@ -212,6 +251,8 @@
 
         @pl.when(slab < n_slab - 1)
         def _():
+            if turn_is_later:
+                top_copy(turn - 1).wait_send()
             top_copy(turn).start()
 
     def exported(state):
@@ -224,6 +265,21 @@
     by_node = jnp.where(
         iota((E, E), 1) == (iota((E, E), 0) & 3) * 64 + (iota((E, E), 0) >> 2), 1.0, 0.0
     ).astype(BF16)
+    loads[5].wait()
+    loads[6].wait()
+    codes[...] = jnp.zeros((32, E), F32)
+    codes[0:6, :] = (v_links[...] >> 8).astype(F32)
+    codes[8:14, :] = (v_links[...] & 255).astype(F32)
+    codes[16:22, :] = v_orient[...].astype(F32)
+    codes[24:25, :] = (v_exports[...] >> 8).astype(F32)
+    moved = dot(codes[0:24, :].astype(BF16), select[...])
+    out_link = moved[0:8, :] * 256.0 + moved[8:16, :]
+    for way in range(2):
+        at = slice(way * PEER, way * PEER + PEER)
+        far_send[way, 0:8, :] = out_link[:, at]
+        far_send[way, 8:16, :] = moved[16:24, at]
+        far_send[way, 16:24, :] = codes[24:32, at]
+    turn_out_rows = moved[16:24, :].astype(jnp.int32)
     loads[1].wait()
     loads[2].wait()
     time_high, time_low = halves(v_lift_time[...].T)
@@ -238,33 +294,29 @@
     first = dot(inv_node[:E, :], rhs_high) + dot(inv_node[:E, :], rhs_low) + dot(inv_node[E:, :], rhs_high)
     const_node[...] = first
     leaving = exported(first)
-    count = jnp.where(slab > 0, 1, 0) + jnp.where(slab < n_slab - 1, 1, 0) + 2
+    count = jnp.where(slab > 0, 1, 0) + jnp.where(slab < n_slab - 1, 1, 0) + 4
     pl.semaphore_wait(barrier, count)
-    send_out(0, leaving)
-    keep(0, first)
-
-    loads[5].wait()
-    loads[6].wait()
-    codes[...] = jnp.zeros((32, E), F32)
-    codes[0:6, :] = (v_links[...] >> 8).astype(F32)
-    codes[8:14, :] = (v_links[...] & 255).astype(F32)
-    codes[16:22, :] = v_orient[...].astype(F32)
-    moved = dot(codes[...].astype(BF16), select[...])
-    far_link = (moved[0:8, :] * 256.0 + moved[8:16, :]).astype(jnp.int32)
-    far_turn = moved[16:24, :].astype(jnp.int32)
+    send_out(0, leaving, False)
+    for copy in far_copies + skip_copies:
+        copy.start()
+    keep(0, first, False)
+
     for face in range(6):
         at = slice(face * E, face * E + E)
         link_rows[:, at] = jnp.broadcast_to(v_links[face : face + 1, :], (16, E))
         turn_rows[face] = jnp.broadcast_to(v_orient[face : face + 1, :], (8, E))
-        turn_out[face] = jnp.broadcast_to(far_turn[face : face + 1, :], (8, E))
-        wanted = jnp.broadcast_to(far_link[face : face + 1, :], (2 * PEER, E))
+        turn_out[face] = jnp.broadcast_to(turn_out_rows[face : face + 1, :], (8, E))
+        wanted = jnp.broadcast_to(out_link[face : face + 1, :].astype(jnp.int32), (2 * PEER, E))
         pick_near[:, at] = jnp.where(wanted == iota((2 * PEER, E), 0) + LOCAL, 1.0, 0.0).astype(BF16)
 
-    @pl.loop(0, TABLE // 16)
-    def _(step):
-        row = pl.multiple_of(step * 16, 16)
-        hit = link_rows[...] == iota((16, LOCAL), 0) + row
-        pick[pl.ds(row, 16), :] = jnp.where(hit, 1.0, 0.0).astype(BF16)
+    @pl.loop(0, TABLE // E)
+    def _(tile):
+        keys = jnp.where(link_rows[...] >> 8 == tile, link_rows[...] & 255, -1).astype(F32).astype(BF16)
+        one, zero = jnp.ones((16, LOCAL), BF16), jnp.zeros((16, LOCAL), BF16)
+        for step in range(E // 16):
+            row = (iota((16, LOCAL), 0) + step * 16).astype(F32).astype(BF16)
+            at = pl.multiple_of(tile * E + step * 16, 16)
+            pick[pl.ds(at, 16), :] = jnp.where(keys == row, one, zero)
 
     column = iota((512, K), 1)
     face_source = ((column & 3) * 16 + ((column >> 3) & 15)) * 6 + (column >> 7)
@@ -320,27 +372,76 @@
             copy.wait_recv()
         for way in range(2):
             for half in range(8):
-                pair = split_pair(arrived[turn, way, half * 8 : half * 8 + 8, :])
+                rows = slice(half * 8, half * 8 + 8)
+                pair = split_pair(arrived[turn, way, rows, :] + extra[way, rows, :])
                 table[
                     half * 16 : half * 16 + 16, LOCAL + way * PEER : LOCAL + way * PEER + PEER
                 ] = jnp.concatenate(pair, axis=0).astype(BF16)
 
-    def remote_part(lhs, chosen, base, turns):
+    def remote_part(chosen, base, turns, columns=lambda: table[:, LOCAL:], depth=2 * PEER):
         for face in range(6):
             at = slice(face * E, face * E + E)
-            block = dot(table[:, LOCAL:], chosen[base : base + 2 * PEER, at])
+            block = dot(columns(), chosen[base : base + depth, at])
             store_rows(nbr_far, face, oriented(block, turns[face]))
-        return dot(lhs[:E, :NBR], nbr_far[...]) + dot(lhs[E:, :NBR], nbr_far[...])
-
-    @pl.loop(0, ROUNDS - 1)
-    def _(turn):
+
+
+    def local_sums(turn):
         local_part(turn)
-        so_far = const_node[...] + dot(lhs_node[:E, :], nbr[...]) + dot(lhs_node[E:, :], nbr[...])
+        so_far = const_node[...] + apply(lhs_node, nbr, K)
         own[...] = so_far
         own_out[...] = exported(so_far)
+
+    def update(turn):
+        @pl.when(space >= 0)
+        def _():
+            remote_part(pick, LOCAL, turn_rows)
+
+        @pl.when(slab >= 0)
+        def _():
+            keep(turn + 1, own[...] + apply(lhs_node, nbr_far, NBR))
+
+    extra[...] = jnp.zeros((2, 64, PEER), F32)
+    local_sums(0)
+    send_out(1, own_out[...])
+    receive(0)
+    update(0)
+
+    for copy in far_copies + skip_copies:
+        copy.wait_recv()
+    side = jnp.where(iota((8, E), 1) < PEER, 0, 2 * PEER)
+    for face in range(6):
+        at = slice(face * E, face * E + E)
+        link = jnp.concatenate([far_arrived[way, face : face + 1, :] for way in range(2)], axis=1).astype(jnp.int32)
+        turned = jnp.concatenate([far_arrived[way, 8 + face : 9 + face, :] for way in range(2)], axis=1)
+        far_turn[face] = jnp.broadcast_to(turned.astype(jnp.int32), (8, E))
+        row = jnp.where(link >= LOCAL, link - LOCAL + side[0:1, :], -1)
+        wanted = jnp.broadcast_to(row, (4 * PEER, E))
+        far_pick[:, at] = jnp.where(wanted == iota((4 * PEER, E), 0), 1.0, 0.0).astype(BF16)
+    for at, part in enumerate((skip_arrived.at[0], send.at[0, 0], send.at[0, 1], skip_arrived.at[1])):
+        for half in range(8):
+            pair = split_pair(part[half * 8 : half * 8 + 8, :])
+            far_table[half * 16 : half * 16 + 16, at * PEER : at * PEER + PEER] = jnp.concatenate(
+                pair, axis=0
+            ).astype(BF16)
+    remote_part(far_pick, 0, far_turn, lambda: far_table[...], 4 * PEER)
+    face_code = jnp.concatenate([far_arrived[way, 16:17, :] for way in range(2)], axis=1).astype(jnp.int32)
+    added = face_traces(apply(lhs_node, nbr_far, NBR), jnp.broadcast_to(face_code, (8, E)))
+    for half, rows in enumerate(added):
+        extra[0, half * 8 : half * 8 + 8, :] = rows[:, :PEER]
+        extra[1, half * 8 : half * 8 + 8, :] = rows[:, PEER:]
+
+    @pl.loop(1, ROUNDS - 1)
+    def _(turn):
+        local_sums(turn)
         receive(turn)
-        send_out(turn + 1, own_out[...] + remote_part(lhs_node, pick_near, 0, turn_out))
-        keep(turn + 1, own[...] + remote_part(lhs_node, pick, LOCAL, turn_rows))
+        extra[...] = jnp.zeros((2, 64, PEER), F32)
+        remote_part(pick_near, 0, turn_out)
+
+        @pl.when(slab >= 0)
+        def _():
+            send_out(turn + 1, own_out[...] + apply(lhs_node, nbr_far, NBR))
+
+        update(turn)
 
     inv_high, inv_low = halves(v_inverse[...])
     rhs_high, rhs_low = halves(v_source[...] + jnp.where(slab == 0, start, 0.0))
@@ -349,18 +450,20 @@
     lhs_time[:E, :] = time_high
     lhs_time[E:, :] = time_low
     local_part(ROUNDS - 1)
-    own[...] += dot(lhs_time[:E, :], nbr[...]) + dot(lhs_time[E:, :], nbr[...])
+    own[...] += apply(lhs_time, nbr, K)
     receive(ROUNDS - 1)
-    out[0] = own[...] + remote_part(lhs_time, pick, LOCAL, turn_rows)
-
-    @pl.loop(0, ROUNDS)
-    def _(turn):
-        for copy in space_copies(turn):
-            copy.wait_send()
-
-        @pl.when(slab < n_slab - 1)
-        def _():
-            top_copy(turn).wait_send()
+    remote_part(pick, LOCAL, turn_rows)
+
+    @pl.when(slab >= 0)
+    def _():
+        out[0] = own[...] + apply(lhs_time, nbr_far, NBR)
+
+    for copy in space_copies(ROUNDS - 1) + far_copies + skip_copies:
+        copy.wait_send()
+
+    @pl.when(slab < n_slab - 1)
+    def _():
+        top_copy(ROUNDS - 1).wait_send()
 
 
 def body(n_space, n_slab, source, initial, inverse, lift, lift_time, links, orient, exports, counts):
@@ -408,11 +511,20 @@
             vmem((ROUNDS, 2, 64, PEER), F32),
             vmem((ROUNDS, 64, E), F32),
             vmem((ROUNDS, 64, E), F32),
+            vmem((2, 24, PEER), F32),
+            vmem((2, 24, PEER), F32),
+            vmem((2, 64, PEER), F32),
+            vmem((4 * PEER, LOCAL), BF16),
+            vmem((128, 4 * PEER), BF16),
+            vmem((6, 8, E), jnp.int32),
+            vmem((2, 64, PEER), F32),
             dma((8,)),
+            dma((2,)),
             dma((ROUNDS, 2)),
-            dma((ROUNDS, 2)),
+            dma,
             dma((ROUNDS,)),
-            dma((ROUNDS,)),
+            dma((2, 2)),
+            dma((2, 2)),
         ],
         compiler_params=pltpu.CompilerParams(
             collective_id=0, has_side_effects=True, vmem_limit_bytes=48 * 1024 * 1024

time: 35.1 us -> 34.1 us (0.972)
  Pallas kernels: 33.6 us -> 32.6 us
    pallas_call x1, Pallas kernels: 33.6 us -> 32.6 us  [body(): pl.pallas_call(functools.partial(kernel, n_space, n_slab), name='window',...]
where the time goes in v4:
time: 34.1 us; the launch traced here: 34 us
  Pallas kernels  32.6 us (96%)
  other arithmetic  0.73 us (2%)
  between operations  0.67 us (2%)
    pallas_call x1, Pallas kernels, body(): pl.pallas_call(functools.partial(kernel, n_space, n_slab), name='window',...  32.6 us
    select_n x1, other arithmetic, body(): return jnp.where(live[None, None, :], state, 0.0)  0.72 us

profile of v4, /device:TPU:6, one launch (start us, length us, event | category | flops | bytes accessed | tf_op | source)
XLA Modules:
  0.0 34.0 jit_solution(11378847169352521708)
XLA Ops:
  0.7 32.6 %window.1 = f32[1,256,256]{2,1,0:T(8,128)S(1)} custom-call(f32[1,256,256]{2,1,0:T(8,128)} %source.1, f32[64,256]{1,0:T(8,128)} %initial.1, f32[256,256]{1,0:T(8,128)} %inverse.1, f32[256,384]{1,0:T(8,128)} %lift.1, f32[64,256]{1,0:T(8,128)} %bitcast.4, s32[6,256]{1,0:T(8,128)} %links.1, s32[6,256]{1,0:T(8,128)} %orient.1, s32[1,256]{1,0:T(1,128)} %bitcast.5), custom_call_target="tpu_custom_call" | custom-call | tf_op jit(solution)/shard_map/window/pallas_call | solution.py:475
  33.3 0.7 %broadcast_select_fusion = f32[1,256,256]{2,1,0:T(8,128)} fusion(f32[1,256,256]{2,1,0:T(8,128)S(1)} %window.1, pred[256]{0:T(512)(128)(4,1)S(1)} %iota_compare_fusion), kind=kLoop, calls=%fused_computation | loop fusion | flops 65536 | bytes 524544 | tf_op jit(solution)/shard_map/jit(_where)/select_n | solution.py:534
  (1 shorter events, 0.0 us)

commit v5 on v4

--- a/solution.py
+++ b/solution.py
@@ -52,11 +52,12 @@
     return tiles
 
 
-def apply(lhs, rows, depth):
+def apply(lhs, rows, begin, end):
     parts = []
     for at in (0, 128):
         parts.append(
-            dot(lhs[at : at + 128, :depth], rows[...]) + dot(lhs[E + at : E + at + 128, :depth], rows[...])
+            dot(lhs[at : at + 128, begin:end], rows[begin:end, :])
+            + dot(lhs[E + at : E + at + 128, begin:end], rows[begin:end, :])
         )
     return jnp.concatenate(parts, axis=0)
 
@@ -127,6 +128,9 @@
     lhs_time,
     inv_node,
     const_node,
+    const_time,
+    by_node,
+    by_time,
     own,
     own_out,
     lift_all,
@@ -168,12 +172,12 @@
     for at, (src, dst) in enumerate(
         (
             (exports, v_exports),
+            (links, v_links),
+            (orient, v_orient),
             (lift_time, v_lift_time),
             (initial, v_initial),
             (inverse, v_inverse),
             (source.at[0], v_source),
-            (links, v_links),
-            (orient, v_orient),
             (lift, v_lift),
         )
     ):
@@ -259,48 +263,61 @@
         high, low = halves(state)
         return dot(high, select[...]) + dot(low, select[...])
 
-    loads[0].wait()
+    row, column = iota((E, E), 0), iota((E, E), 1)
+    by_node[...] = jnp.where(column == (row & 3) * 64 + (row >> 2), 1.0, 0.0).astype(BF16)
+    by_time[...] = jnp.where(column == (row & 63) * 4 + (row >> 6), 1.0, 0.0).astype(BF16)
+    column = iota((512, K), 1)
+    face_source = ((column & 3) * 16 + ((column >> 3) & 15)) * 6 + (column >> 7)
+    wanted_row = jnp.where(column < NBR, face_source, 384 + (column & 63))
+    spread[...] = jnp.where(iota((512, K), 0) == wanted_row, 1.0, 0.0).astype(BF16)
+    codes[...] = jnp.zeros((32, E), F32)
+    extra[...] = jnp.zeros((2, 64, PEER), F32)
+    nbr[NBR:, :] = jnp.zeros((128, E), BF16)
+    lift_all[:, 384:] = jnp.zeros((E, 128), F32)
+
+    for load in loads[:6]:
+        load.wait()
     element = jnp.broadcast_to(v_exports[...] & 255, (E, E))
     select[...] = jnp.where(element == iota((E, E), 0), 1.0, 0.0).astype(BF16)
-    by_node = jnp.where(
-        iota((E, E), 1) == (iota((E, E), 0) & 3) * 64 + (iota((E, E), 0) >> 2), 1.0, 0.0
-    ).astype(BF16)
-    loads[5].wait()
-    loads[6].wait()
-    codes[...] = jnp.zeros((32, E), F32)
     codes[0:6, :] = (v_links[...] >> 8).astype(F32)
     codes[8:14, :] = (v_links[...] & 255).astype(F32)
     codes[16:22, :] = v_orient[...].astype(F32)
     codes[24:25, :] = (v_exports[...] >> 8).astype(F32)
     moved = dot(codes[0:24, :].astype(BF16), select[...])
+    time_high, time_low = halves(v_lift_time[...].T)
+    first_high, first_low = halves(v_initial[...])
+    start = dot(time_high, first_high) + dot(time_high, first_low) + dot(time_low, first_high)
+    inv_high, inv_low = halves(v_inverse[...])
+    inv_node[:E, :] = dot(by_node[...], inv_high).astype(BF16)
+    inv_node[E:, :] = dot(by_node[...], inv_low).astype(BF16)
     out_link = moved[0:8, :] * 256.0 + moved[8:16, :]
     for way in range(2):
         at = slice(way * PEER, way * PEER + PEER)
         far_send[way, 0:8, :] = out_link[:, at]
         far_send[way, 8:16, :] = moved[16:24, at]
         far_send[way, 16:24, :] = codes[24:32, at]
-    turn_out_rows = moved[16:24, :].astype(jnp.int32)
-    loads[1].wait()
-    loads[2].wait()
-    time_high, time_low = halves(v_lift_time[...].T)
-    first_high, first_low = halves(v_initial[...])
-    start = dot(time_high, first_high) + dot(time_high, first_low) + dot(time_low, first_high)
-    loads[3].wait()
-    inv_high, inv_low = halves(v_inverse[...])
-    inv_node[:E, :] = dot(by_node, inv_high).astype(BF16)
-    inv_node[E:, :] = dot(by_node, inv_low).astype(BF16)
-    loads[4].wait()
+    count = jnp.where(slab > 0, 1, 0) + jnp.where(slab < n_slab - 1, 1, 0) + 4
+    pl.semaphore_wait(barrier, count)
+    for copy in far_copies:
+        copy.start()
+    loads[6].wait()
     rhs_high, rhs_low = halves(v_source[...] + jnp.where(slab == 0, start, 0.0))
     first = dot(inv_node[:E, :], rhs_high) + dot(inv_node[:E, :], rhs_low) + dot(inv_node[E:, :], rhs_high)
     const_node[...] = first
     leaving = exported(first)
-    count = jnp.where(slab > 0, 1, 0) + jnp.where(slab < n_slab - 1, 1, 0) + 4
-    pl.semaphore_wait(barrier, count)
     send_out(0, leaving, False)
-    for copy in far_copies + skip_copies:
+    for copy in skip_copies:
         copy.start()
     keep(0, first, False)
 
+    turn_out_rows = moved[16:24, :].astype(jnp.int32)
+    loads[7].wait()
+    lift_all[:, :384] = v_lift[...]
+    lift_all[:, 384:448] = v_lift_time[...].T
+    lift_high, lift_low = halves(lift_all[...])
+    node_high, node_low = halves(
+        dot(inv_node[:E, :], lift_high) + dot(inv_node[:E, :], lift_low) + dot(inv_node[E:, :], lift_high)
+    )
     for face in range(6):
         at = slice(face * E, face * E + E)
         link_rows[:, at] = jnp.broadcast_to(v_links[face : face + 1, :], (16, E))
@@ -308,37 +325,20 @@
         turn_out[face] = jnp.broadcast_to(turn_out_rows[face : face + 1, :], (8, E))
         wanted = jnp.broadcast_to(out_link[face : face + 1, :].astype(jnp.int32), (2 * PEER, E))
         pick_near[:, at] = jnp.where(wanted == iota((2 * PEER, E), 0) + LOCAL, 1.0, 0.0).astype(BF16)
-
-    @pl.loop(0, TABLE // E)
-    def _(tile):
-        keys = jnp.where(link_rows[...] >> 8 == tile, link_rows[...] & 255, -1).astype(F32).astype(BF16)
-        one, zero = jnp.ones((16, LOCAL), BF16), jnp.zeros((16, LOCAL), BF16)
-        for step in range(E // 16):
-            row = (iota((16, LOCAL), 0) + step * 16).astype(F32).astype(BF16)
-            at = pl.multiple_of(tile * E + step * 16, 16)
-            pick[pl.ds(at, 16), :] = jnp.where(keys == row, one, zero)
-
-    column = iota((512, K), 1)
-    face_source = ((column & 3) * 16 + ((column >> 3) & 15)) * 6 + (column >> 7)
-    wanted_row = jnp.where(column < NBR, face_source, 384 + (column & 63))
-    spread[...] = jnp.where(iota((512, K), 0) == wanted_row, 1.0, 0.0).astype(BF16)
-    loads[7].wait()
-    lift_all[:, :384] = v_lift[...]
-    lift_all[:, 384:] = jnp.zeros((E, 128), F32)
-    lift_all[:, 384:448] = v_lift_time[...].T
-    lift_high, lift_low = halves(lift_all[...])
-    lhs_time[:E, :] = dot(lift_high, spread[...]).astype(BF16)
-    lhs_time[E:, :] = dot(lift_low, spread[...]).astype(BF16)
-
-    def operator(high, low):
-        return halves(dot(high, lhs_time[:E, :]) + dot(high, lhs_time[E:, :]) + dot(low, lhs_time[:E, :]))
-
-    node_high, node_low = operator(inv_node[:E, :], inv_node[E:, :])
-    lhs_node[:E, :] = node_high
-    lhs_node[E:, :] = node_low
-    nbr[NBR:, :] = jnp.zeros((128, E), BF16)
-
-    def local_part(turn):
+    one, zero = jnp.ones((16, E), BF16), jnp.zeros((16, E), BF16)
+    for face in range(6):
+        at = slice(face * E, face * E + E)
+        for tile in range(TABLE // E):
+            link = link_rows[:, at]
+            keys = jnp.where(link >> 8 == tile, link & 255, -1).astype(F32).astype(BF16)
+            for step in range(E // 16):
+                row = (iota((16, E), 0) + step * 16).astype(F32).astype(BF16)
+                base = tile * E + step * 16
+                pick[base : base + 16, at] = jnp.where(keys == row, one, zero)
+    lhs_node[:E, :] = dot(node_high, spread[...]).astype(BF16)
+    lhs_node[E:, :] = dot(node_low, spread[...]).astype(BF16)
+
+    def local_part(turn, lhs, const):
         for pair in range(32):
             for half in range(2):
                 at = slice(half * 128, half * 128 + 128)
@@ -354,6 +354,7 @@
         for face in range(6):
             at = slice(face * E, face * E + E)
             store_rows(nbr, face, oriented(dot(table[:, :LOCAL], pick[:LOCAL, at]), turn_rows[face]))
+        sums = const[...] + apply(lhs, nbr, 0, NBR)
 
         @pl.when(slab > 0)
         def _():
@@ -361,6 +362,8 @@
             high, low = halves(top_arrived[turn])
             nbr[NBR : NBR + 64, :] = high
             nbr[NBR + 64 :, :] = low
+
+        return sums + apply(lhs, nbr, NBR, K)
 
     def store_rows(ref, face, tiles):
         for half in range(8):
@@ -379,15 +382,14 @@
                 ] = jnp.concatenate(pair, axis=0).astype(BF16)
 
     def remote_part(chosen, base, turns, columns=lambda: table[:, LOCAL:], depth=2 * PEER):
-        for face in range(6):
-            at = slice(face * E, face * E + E)
-            block = dot(columns(), chosen[base : base + depth, at])
-            store_rows(nbr_far, face, oriented(block, turns[face]))
+        for face in (0, 2, 4):
+            block = dot(columns(), chosen[base : base + depth, face * E : face * E + 2 * E])
+            store_rows(nbr_far, face, oriented(block[:, :E], turns[face]))
+            store_rows(nbr_far, face + 1, oriented(block[:, E:], turns[face + 1]))
 
 
     def local_sums(turn):
-        local_part(turn)
-        so_far = const_node[...] + apply(lhs_node, nbr, K)
+        so_far = local_part(turn, lhs_node, const_node)
         own[...] = so_far
         own_out[...] = exported(so_far)
 
@@ -398,15 +400,11 @@
 
         @pl.when(slab >= 0)
         def _():
-            keep(turn + 1, own[...] + apply(lhs_node, nbr_far, NBR))
-
-    extra[...] = jnp.zeros((2, 64, PEER), F32)
+            keep(turn + 1, own[...] + apply(lhs_node, nbr_far, 0, NBR))
+
     local_sums(0)
     send_out(1, own_out[...])
-    receive(0)
-    update(0)
-
-    for copy in far_copies + skip_copies:
+    for copy in far_copies:
         copy.wait_recv()
     side = jnp.where(iota((8, E), 1) < PEER, 0, 2 * PEER)
     for face in range(6):
@@ -417,6 +415,10 @@
         row = jnp.where(link >= LOCAL, link - LOCAL + side[0:1, :], -1)
         wanted = jnp.broadcast_to(row, (4 * PEER, E))
         far_pick[:, at] = jnp.where(wanted == iota((4 * PEER, E), 0), 1.0, 0.0).astype(BF16)
+    receive(0)
+    update(0)
+    for copy in skip_copies:
+        copy.wait_recv()
     for at, part in enumerate((skip_arrived.at[0], send.at[0, 0], send.at[0, 1], skip_arrived.at[1])):
         for half in range(8):
             pair = split_pair(part[half * 8 : half * 8 + 8, :])
@@ -425,7 +427,7 @@
             ).astype(BF16)
     remote_part(far_pick, 0, far_turn, lambda: far_table[...], 4 * PEER)
     face_code = jnp.concatenate([far_arrived[way, 16:17, :] for way in range(2)], axis=1).astype(jnp.int32)
-    added = face_traces(apply(lhs_node, nbr_far, NBR), jnp.broadcast_to(face_code, (8, E)))
+    added = face_traces(apply(lhs_node, nbr_far, 0, NBR), jnp.broadcast_to(face_code, (8, E)))
     for half, rows in enumerate(added):
         extra[0, half * 8 : half * 8 + 8, :] = rows[:, :PEER]
         extra[1, half * 8 : half * 8 + 8, :] = rows[:, PEER:]
@@ -439,24 +441,21 @@
 
         @pl.when(slab >= 0)
         def _():
-            send_out(turn + 1, own_out[...] + apply(lhs_node, nbr_far, NBR))
+            send_out(turn + 1, own_out[...] + apply(lhs_node, nbr_far, 0, NBR))
 
         update(turn)
 
-    inv_high, inv_low = halves(v_inverse[...])
-    rhs_high, rhs_low = halves(v_source[...] + jnp.where(slab == 0, start, 0.0))
-    own[...] = dot(inv_high, rhs_high) + dot(inv_high, rhs_low) + dot(inv_low, rhs_high)
-    time_high, time_low = operator(inv_high, inv_low)
-    lhs_time[:E, :] = time_high
-    lhs_time[E:, :] = time_low
-    local_part(ROUNDS - 1)
-    own[...] += apply(lhs_time, nbr, K)
+    lhs_time[:E, :] = dot(by_time[...], lhs_node[:E, :]).astype(BF16)
+    lhs_time[E:, :] = dot(by_time[...], lhs_node[E:, :]).astype(BF16)
+    high, low = halves(const_node[...])
+    const_time[...] = dot(by_time[...], high) + dot(by_time[...], low)
+    own[...] = local_part(ROUNDS - 1, lhs_time, const_time)
     receive(ROUNDS - 1)
     remote_part(pick, LOCAL, turn_rows)
 
     @pl.when(slab >= 0)
     def _():
-        out[0] = own[...] + apply(lhs_time, nbr_far, NBR)
+        out[0] = own[...] + apply(lhs_time, nbr_far, 0, NBR)
 
     for copy in space_copies(ROUNDS - 1) + far_copies + skip_copies:
         copy.wait_send()
@@ -496,6 +495,9 @@
             vmem((512, K), BF16),
             vmem((512, 256), BF16),
             vmem((256, E), F32),
+            vmem((256, E), F32),
+            vmem((256, 256), BF16),
+            vmem((256, 256), BF16),
             vmem((256, E), F32),
             vmem((256, E), F32),
             vmem((256, 512), F32),

time: 34.1 us -> 33.9 us (level)
  no operation moved by 1% of the time
where the time goes in v5:
time: 33.9 us; the launch traced here: 33.8 us
  Pallas kernels  32.4 us (96%)
  other arithmetic  0.73 us (2%)
  between operations  0.67 us (2%)
    pallas_call x1, Pallas kernels, body(): pl.pallas_call(functools.partial(kernel, n_space, n_slab), name='window',...  32.4 us
    select_n x1, other arithmetic, body(): return jnp.where(live[None, None, :], state, 0.0)  0.72 us

profile of v5, /device:TPU:6, one launch (start us, length us, event | category | flops | bytes accessed | tf_op | source)
XLA Modules:
  0.0 33.8 jit_solution(9976138144053739142)
XLA Ops:
  0.7 32.4 %window.1 = f32[1,256,256]{2,1,0:T(8,128)S(1)} custom-call(f32[1,256,256]{2,1,0:T(8,128)} %source.1, f32[64,256]{1,0:T(8,128)} %initial.1, f32[256,256]{1,0:T(8,128)} %inverse.1, f32[256,384]{1,0:T(8,128)} %lift.1, f32[64,256]{1,0:T(8,128)} %bitcast.4, s32[6,256]{1,0:T(8,128)} %links.1, s32[6,256]{1,0:T(8,128)} %orient.1, s32[1,256]{1,0:T(1,128)} %bitcast.5), custom_call_target="tpu_custom_call" | custom-call | tf_op jit(solution)/shard_map/window/pallas_call | solution.py:474
  33.0 0.7 %broadcast_select_fusion = f32[1,256,256]{2,1,0:T(8,128)} fusion(f32[1,256,256]{2,1,0:T(8,128)S(1)} %window.1, pred[256]{0:T(512)(128)(4,1)S(1)} %iota_compare_fusion), kind=kLoop, calls=%fused_computation | loop fusion | flops 65536 | bytes 524544 | tf_op jit(solution)/shard_map/jit(_where)/select_n | solution.py:536
  (1 shorter events, 0.0 us)

commit v6 on v5

--- a/solution.py
+++ b/solution.py
@@ -241,9 +241,10 @@
         for half, rows in enumerate(face_traces(state, code)):
             send[turn, 0, half * 8 : half * 8 + 8, :] = rows[:, :PEER]
             send[turn, 1, half * 8 : half * 8 + 8, :] = rows[:, PEER:]
-        if turn_is_later:
-            for copy in space_copies(turn - 1):
-                copy.wait_send()
+        if not turn_is_later:
+            return
+        for copy in space_copies(turn - 1):
+            copy.wait_send()
         for copy in space_copies(turn):
             copy.start()
 
@@ -252,11 +253,12 @@
             fresh[half] = state[:, half * 128 : half * 128 + 128]
         for half in range(2):
             top_send[turn, :, half * 128 : half * 128 + 128] = fresh[half, pl.ds(3, 64, stride=4), :]
+        if not turn_is_later:
+            return
 
         @pl.when(slab < n_slab - 1)
         def _():
-            if turn_is_later:
-                top_copy(turn - 1).wait_send()
+            top_copy(turn - 1).wait_send()
             top_copy(turn).start()
 
     def exported(state):
@@ -271,8 +273,8 @@
     wanted_row = jnp.where(column < NBR, face_source, 384 + (column & 63))
     spread[...] = jnp.where(iota((512, K), 0) == wanted_row, 1.0, 0.0).astype(BF16)
     codes[...] = jnp.zeros((32, E), F32)
-    extra[...] = jnp.zeros((2, 64, PEER), F32)
     nbr[NBR:, :] = jnp.zeros((128, E), BF16)
+    nbr_far[NBR:, :] = jnp.zeros((128, E), BF16)
     lift_all[:, 384:] = jnp.zeros((E, 128), F32)
 
     for load in loads[:6]:
@@ -296,19 +298,24 @@
         far_send[way, 0:8, :] = out_link[:, at]
         far_send[way, 8:16, :] = moved[16:24, at]
         far_send[way, 16:24, :] = codes[24:32, at]
-    count = jnp.where(slab > 0, 1, 0) + jnp.where(slab < n_slab - 1, 1, 0) + 4
-    pl.semaphore_wait(barrier, count)
-    for copy in far_copies:
-        copy.start()
     loads[6].wait()
     rhs_high, rhs_low = halves(v_source[...] + jnp.where(slab == 0, start, 0.0))
     first = dot(inv_node[:E, :], rhs_high) + dot(inv_node[:E, :], rhs_low) + dot(inv_node[E:, :], rhs_high)
     const_node[...] = first
     leaving = exported(first)
+    keep(0, first, False)
     send_out(0, leaving, False)
-    for copy in skip_copies:
+    count = jnp.where(slab > 0, 1, 0) + jnp.where(slab < n_slab - 1, 1, 0) + 4
+    pl.semaphore_wait(barrier, count)
+    for copy in space_copies(0):
         copy.start()
-    keep(0, first, False)
+
+    @pl.when(slab < n_slab - 1)
+    def _():
+        top_copy(0).start()
+
+    for copy in far_copies + skip_copies:
+        copy.start()
 
     turn_out_rows = moved[16:24, :].astype(jnp.int32)
     loads[7].wait()
@@ -354,29 +361,31 @@
         for face in range(6):
             at = slice(face * E, face * E + E)
             store_rows(nbr, face, oriented(dot(table[:, :LOCAL], pick[:LOCAL, at]), turn_rows[face]))
-        sums = const[...] + apply(lhs, nbr, 0, NBR)
-
+        return const[...] + apply(lhs, nbr, 0, NBR)
+
+    def take_top(turn, for_exports=False):
         @pl.when(slab > 0)
         def _():
             top_copy(turn).wait_recv()
             high, low = halves(top_arrived[turn])
             nbr[NBR : NBR + 64, :] = high
             nbr[NBR + 64 :, :] = low
-
-        return sums + apply(lhs, nbr, NBR, K)
+            if for_exports:
+                nbr_far[NBR:, :] = dot(nbr[NBR:, :], select[...]).astype(BF16)
 
     def store_rows(ref, face, tiles):
         for half in range(8):
             row = face * 128 + half * 16
             ref[row : row + 16, :] = jnp.concatenate(tiles[2 * half : 2 * half + 2], axis=0).astype(BF16)
 
-    def receive(turn):
+    def receive(turn, completed=False):
         for copy in space_copies(turn):
             copy.wait_recv()
         for way in range(2):
             for half in range(8):
                 rows = slice(half * 8, half * 8 + 8)
-                pair = split_pair(arrived[turn, way, rows, :] + extra[way, rows, :])
+                value = arrived[turn, way, rows, :]
+                pair = split_pair(value + extra[way, rows, :] if completed else value)
                 table[
                     half * 16 : half * 16 + 16, LOCAL + way * PEER : LOCAL + way * PEER + PEER
                 ] = jnp.concatenate(pair, axis=0).astype(BF16)
@@ -388,19 +397,24 @@
             store_rows(nbr_far, face + 1, oriented(block[:, E:], turns[face + 1]))
 
 
-    def local_sums(turn):
+    def local_sums(turn, top_later=False):
         so_far = local_part(turn, lhs_node, const_node)
+        if not top_later:
+            take_top(turn)
+            so_far += apply(lhs_node, nbr, NBR, K)
         own[...] = so_far
         own_out[...] = exported(so_far)
 
-    def update(turn):
+    def update(turn, depth=NBR):
         @pl.when(space >= 0)
         def _():
             remote_part(pick, LOCAL, turn_rows)
+            if depth > NBR:
+                nbr_far[NBR:, :] = nbr[NBR:, :]
 
         @pl.when(slab >= 0)
         def _():
-            keep(turn + 1, own[...] + apply(lhs_node, nbr_far, 0, NBR))
+            keep(turn + 1, own[...] + apply(lhs_node, nbr_far, 0, depth))
 
     local_sums(0)
     send_out(1, own_out[...])
@@ -432,24 +446,33 @@
         extra[0, half * 8 : half * 8 + 8, :] = rows[:, :PEER]
         extra[1, half * 8 : half * 8 + 8, :] = rows[:, PEER:]
 
-    @pl.loop(1, ROUNDS - 1)
-    def _(turn):
-        local_sums(turn)
-        receive(turn)
-        extra[...] = jnp.zeros((2, 64, PEER), F32)
+    def advance(turn, top_later=False):
+        depth = K if top_later else NBR
+        local_sums(turn, top_later)
+        receive(turn, top_later)
         remote_part(pick_near, 0, turn_out)
+        if top_later:
+            take_top(turn, True)
 
         @pl.when(slab >= 0)
         def _():
-            send_out(turn + 1, own_out[...] + apply(lhs_node, nbr_far, 0, NBR))
-
-        update(turn)
+            send_out(turn + 1, own_out[...] + apply(lhs_node, nbr_far, 0, depth))
+
+        update(turn, depth)
+
+    advance(1, True)
+
+    @pl.loop(2, ROUNDS - 1)
+    def _(turn):
+        advance(turn)
 
     lhs_time[:E, :] = dot(by_time[...], lhs_node[:E, :]).astype(BF16)
     lhs_time[E:, :] = dot(by_time[...], lhs_node[E:, :]).astype(BF16)
     high, low = halves(const_node[...])
     const_time[...] = dot(by_time[...], high) + dot(by_time[...], low)
     own[...] = local_part(ROUNDS - 1, lhs_time, const_time)
+    take_top(ROUNDS - 1)
+    own[...] += apply(lhs_time, nbr, NBR, K)
     receive(ROUNDS - 1)
     remote_part(pick, LOCAL, turn_rows)
 
@@ -490,7 +513,7 @@
             vmem((2 * PEER, LOCAL), BF16),
             vmem((128, TABLE), BF16),
             vmem((K, E), BF16),
-            vmem((NBR, E), BF16),
+            vmem((K, E), BF16),
             vmem((512, K), BF16),
             vmem((512, K), BF16),
             vmem((512, 256), BF16),

time: 33.9 us -> 33.5 us (0.988)
  Pallas kernels: 32.4 us -> 32 us
    pallas_call x1, Pallas kernels: 32.4 us -> 32 us  [body(): pl.pallas_call(functools.partial(kernel, n_space, n_slab), name='window',...]
where the time goes in v6:
time: 33.5 us; the launch traced here: 33.4 us
  Pallas kernels  32 us (96%)
  other arithmetic  0.73 us (2%)
  between operations  0.67 us (2%)
    pallas_call x1, Pallas kernels, body(): pl.pallas_call(functools.partial(kernel, n_space, n_slab), name='window',...  32 us
    select_n x1, other arithmetic, body(): return jnp.where(live[None, None, :], state, 0.0)  0.72 us

profile of v6, /device:TPU:6, one launch (start us, length us, event | category | flops | bytes accessed | tf_op | source)
XLA Modules:
  0.0 33.4 jit_solution(16722105185968724355)
XLA Ops:
  0.7 32.0 %window.1 = f32[1,256,256]{2,1,0:T(8,128)S(1)} custom-call(f32[1,256,256]{2,1,0:T(8,128)} %source.1, f32[64,256]{1,0:T(8,128)} %initial.1, f32[256,256]{1,0:T(8,128)} %inverse.1, f32[256,384]{1,0:T(8,128)} %lift.1, f32[64,256]{1,0:T(8,128)} %bitcast.4, s32[6,256]{1,0:T(8,128)} %links.1, s32[6,256]{1,0:T(8,128)} %orient.1, s32[1,256]{1,0:T(1,128)} %bitcast.5), custom_call_target="tpu_custom_call" | custom-call | tf_op jit(solution)/shard_map/window/pallas_call | solution.py:497
  32.7 0.7 %broadcast_select_fusion = f32[1,256,256]{2,1,0:T(8,128)} fusion(f32[1,256,256]{2,1,0:T(8,128)S(1)} %window.1, pred[256]{0:T(512)(128)(4,1)S(1)} %iota_compare_fusion), kind=kLoop, calls=%fused_computation | loop fusion | flops 65536 | bytes 524544 | tf_op jit(solution)/shard_map/jit(_where)/select_n | solution.py:559
  (1 shorter events, 0.0 us)

commit v7 on v6

--- a/solution.py
+++ b/solution.py
@@ -165,8 +165,6 @@
     slab = lax.axis_index("slab")
     upper = {"space": lax.rem(space + 1, n_space)}
     lower = {"space": lax.rem(space + n_space - 1, n_space)}
-    second_upper = {"space": lax.rem(space + 2, n_space)}
-    second_lower = {"space": lax.rem(space + n_space - 2, n_space)}
 
     loads = []
     for at, (src, dst) in enumerate(
@@ -186,7 +184,7 @@
         loads.append(copy)
 
     barrier = pltpu.get_barrier_semaphore()
-    for peer in (lower, upper, second_lower, second_upper):
+    for peer in (lower, upper):
         pl.semaphore_signal(barrier, inc=1, device_id=peer, device_id_type=MESH)
 
     @pl.when(slab > 0)
@@ -224,7 +222,28 @@
         ]
 
     far_copies = other_copies(lambda way: far_send.at[way], far_arrived, far_sem, (lower, upper))
-    skip_copies = other_copies(lambda way: send.at[0, way], skip_arrived, skip_sem, (second_lower, second_upper))
+
+    def first_arrival(side):
+        return pltpu.make_async_remote_copy(
+            src_ref=send.at[0, 1 - side],
+            dst_ref=arrived.at[0, side],
+            send_sem=send_sem.at[1 - side],
+            recv_sem=recv_sem.at[0, side],
+            device_id=lower,
+            device_id_type=MESH,
+        )
+
+    def relay(side):
+        return pltpu.make_async_remote_copy(
+            src_ref=arrived.at[0, side],
+            dst_ref=skip_arrived.at[side],
+            send_sem=skip_sem.at[0, side],
+            recv_sem=skip_sem.at[1, side],
+            device_id={"space": lax.rem(space + n_space + 1 - 2 * side, n_space)},
+            device_id_type=MESH,
+        )
+
+    near_side = lax.rem(space + 1, 2)
 
     def top_copy(turn):
         return pltpu.make_async_remote_copy(
@@ -305,7 +324,7 @@
     leaving = exported(first)
     keep(0, first, False)
     send_out(0, leaving, False)
-    count = jnp.where(slab > 0, 1, 0) + jnp.where(slab < n_slab - 1, 1, 0) + 4
+    count = jnp.where(slab > 0, 1, 0) + jnp.where(slab < n_slab - 1, 1, 0) + 2
     pl.semaphore_wait(barrier, count)
     for copy in space_copies(0):
         copy.start()
@@ -314,7 +333,7 @@
     def _():
         top_copy(0).start()
 
-    for copy in far_copies + skip_copies:
+    for copy in far_copies:
         copy.start()
 
     turn_out_rows = moved[16:24, :].astype(jnp.int32)
@@ -344,6 +363,8 @@
                 pick[base : base + 16, at] = jnp.where(keys == row, one, zero)
     lhs_node[:E, :] = dot(node_high, spread[...]).astype(BF16)
     lhs_node[E:, :] = dot(node_low, spread[...]).astype(BF16)
+    first_arrival(near_side).wait_recv()
+    relay(near_side).start()
 
     def local_part(turn, lhs, const):
         for pair in range(32):
@@ -379,8 +400,12 @@
             ref[row : row + 16, :] = jnp.concatenate(tiles[2 * half : 2 * half + 2], axis=0).astype(BF16)
 
     def receive(turn, completed=False):
-        for copy in space_copies(turn):
-            copy.wait_recv()
+        if completed is None:
+            first_arrival(1 - near_side).wait_recv()
+            relay(1 - near_side).start()
+        else:
+            for copy in space_copies(turn):
+                copy.wait_recv()
         for way in range(2):
             for half in range(8):
                 rows = slice(half * 8, half * 8 + 8)
@@ -429,10 +454,11 @@
         row = jnp.where(link >= LOCAL, link - LOCAL + side[0:1, :], -1)
         wanted = jnp.broadcast_to(row, (4 * PEER, E))
         far_pick[:, at] = jnp.where(wanted == iota((4 * PEER, E), 0), 1.0, 0.0).astype(BF16)
-    receive(0)
+    receive(0, None)
     update(0)
-    for copy in skip_copies:
-        copy.wait_recv()
+    local_sums(1, True)
+    for side in range(2):
+        relay(side).wait_recv()
     for at, part in enumerate((skip_arrived.at[0], send.at[0, 0], send.at[0, 1], skip_arrived.at[1])):
         for half in range(8):
             pair = split_pair(part[half * 8 : half * 8 + 8, :])
@@ -448,15 +474,22 @@
 
     def advance(turn, top_later=False):
         depth = K if top_later else NBR
-        local_sums(turn, top_later)
+        if not top_later:
+            local_sums(turn)
         receive(turn, top_later)
         remote_part(pick_near, 0, turn_out)
         if top_later:
+
+            @pl.when(space >= 0)
+            def _():
+                own_out[...] += apply(lhs_node, nbr_far, 0, NBR)
+
             take_top(turn, True)
 
         @pl.when(slab >= 0)
         def _():
-            send_out(turn + 1, own_out[...] + apply(lhs_node, nbr_far, 0, depth))
+            begin, end = (NBR, K) if top_later else (0, NBR)
+            send_out(turn + 1, own_out[...] + apply(lhs_node, nbr_far, begin, end))
 
         update(turn, depth)
 
@@ -480,7 +513,7 @@
     def _():
         out[0] = own[...] + apply(lhs_time, nbr_far, 0, NBR)
 
-    for copy in space_copies(ROUNDS - 1) + far_copies + skip_copies:
+    for copy in space_copies(ROUNDS - 1) + far_copies + [relay(0), relay(1)]:
         copy.wait_send()
 
     @pl.when(slab < n_slab - 1)

time: 33.5 us -> 33 us (0.985)
  Pallas kernels: 32 us -> 31.5 us
    pallas_call x1, Pallas kernels: 32 us -> 31.5 us  [body(): pl.pallas_call(functools.partial(kernel, n_space, n_slab), name='window',...]
where the time goes in v7:
time: 33 us; the launch traced here: 32.9 us
  Pallas kernels  31.5 us (95%)
  other arithmetic  0.73 us (2%)
  between operations  0.67 us (2%)
    pallas_call x1, Pallas kernels, body(): pl.pallas_call(functools.partial(kernel, n_space, n_slab), name='window',...  31.5 us
    select_n x1, other arithmetic, body(): return jnp.where(live[None, None, :], state, 0.0)  0.72 us

profile of v7, /device:TPU:6, one launch (start us, length us, event | category | flops | bytes accessed | tf_op | source)
XLA Modules:
  0.0 32.9 jit_solution(8624105806742426082)
XLA Ops:
  0.7 31.5 %window.1 = f32[1,256,256]{2,1,0:T(8,128)S(1)} custom-call(f32[1,256,256]{2,1,0:T(8,128)} %source.1, f32[64,256]{1,0:T(8,128)} %initial.1, f32[256,256]{1,0:T(8,128)} %inverse.1, f32[256,384]{1,0:T(8,128)} %lift.1, f32[64,256]{1,0:T(8,128)} %bitcast.4, s32[6,256]{1,0:T(8,128)} %links.1, s32[6,256]{1,0:T(8,128)} %orient.1, s32[1,256]{1,0:T(1,128)} %bitcast.5), custom_call_target="tpu_custom_call" | custom-call | tf_op jit(solution)/shard_map/window/pallas_call | solution.py:530
  32.2 0.7 %broadcast_select_fusion = f32[1,256,256]{2,1,0:T(8,128)} fusion(f32[1,256,256]{2,1,0:T(8,128)S(1)} %window.1, pred[256]{0:T(512)(128)(4,1)S(1)} %iota_compare_fusion), kind=kLoop, calls=%fused_computation | loop fusion | flops 65536 | bytes 524544 | tf_op jit(solution)/shard_map/jit(_where)/select_n | solution.py:592
  (1 shorter events, 0.0 us)

commit v8 on v7

--- a/solution.py
+++ b/solution.py
@@ -133,6 +133,8 @@
     by_time,
     own,
     own_out,
+    face_out,
+    nbr_near,
     lift_all,
     spread,
     link_rows,
@@ -255,17 +257,24 @@
             device_id_type=MESH,
         )
 
-    def send_out(turn, state, turn_is_later=True):
-        code = jnp.broadcast_to(v_exports[...] >> 8, (8, E))
-        for half, rows in enumerate(face_traces(state, code)):
-            send[turn, 0, half * 8 : half * 8 + 8, :] = rows[:, :PEER]
-            send[turn, 1, half * 8 : half * 8 + 8, :] = rows[:, PEER:]
-        if not turn_is_later:
-            return
-        for copy in space_copies(turn - 1):
-            copy.wait_send()
-        for copy in space_copies(turn):
-            copy.start()
+    def export_copy(turn, way):
+        return pltpu.make_async_remote_copy(
+            src_ref=send.at[turn, way],
+            dst_ref=arrived.at[turn, 1 - way],
+            send_sem=send_sem.at[way],
+            recv_sem=recv_sem.at[turn, 1 - way],
+            device_id={"space": lax.rem(space + n_space - 1 + 2 * way, n_space)},
+            device_id_type=MESH,
+        )
+
+    def fill(turn, way, state):
+        for half, rows in enumerate(face_traces(state, face_out[way])):
+            send[turn, way, half * 8 : half * 8 + 8, :] = rows
+
+    def send_one(turn, way, state):
+        fill(turn, way, state)
+        export_copy(turn - 1, way).wait_send()
+        export_copy(turn, way).start()
 
     def keep(turn, state, turn_is_later=True):
         for half in range(2):
@@ -323,7 +332,10 @@
     const_node[...] = first
     leaving = exported(first)
     keep(0, first, False)
-    send_out(0, leaving, False)
+    for way in range(2):
+        half = slice(way * PEER, way * PEER + PEER)
+        face_out[way] = jnp.broadcast_to(v_exports[:, half] >> 8, (8, PEER))
+        fill(0, way, leaving[:, half])
     count = jnp.where(slab > 0, 1, 0) + jnp.where(slab < n_slab - 1, 1, 0) + 2
     pl.semaphore_wait(barrier, count)
     for copy in space_copies(0):
@@ -348,9 +360,13 @@
         at = slice(face * E, face * E + E)
         link_rows[:, at] = jnp.broadcast_to(v_links[face : face + 1, :], (16, E))
         turn_rows[face] = jnp.broadcast_to(v_orient[face : face + 1, :], (8, E))
-        turn_out[face] = jnp.broadcast_to(turn_out_rows[face : face + 1, :], (8, E))
         wanted = jnp.broadcast_to(out_link[face : face + 1, :].astype(jnp.int32), (2 * PEER, E))
-        pick_near[:, at] = jnp.where(wanted == iota((2 * PEER, E), 0) + LOCAL, 1.0, 0.0).astype(BF16)
+        hit = jnp.where(wanted == iota((2 * PEER, E), 0) + LOCAL, 1.0, 0.0).astype(BF16)
+        code = jnp.broadcast_to(turn_out_rows[face : face + 1, :], (8, E))
+        for way in range(2):
+            half = slice(way * PEER, way * PEER + PEER)
+            pick_near[way, :, face * PEER : face * PEER + PEER] = hit[:, half]
+            turn_out[way, face] = code[:, half]
     one, zero = jnp.ones((16, E), BF16), jnp.zeros((16, E), BF16)
     for face in range(6):
         at = slice(face * E, face * E + E)
@@ -428,7 +444,9 @@
             take_top(turn)
             so_far += apply(lhs_node, nbr, NBR, K)
         own[...] = so_far
-        own_out[...] = exported(so_far)
+        leaving = exported(so_far)
+        own_out[0] = leaving[:, :PEER]
+        own_out[1] = leaving[:, PEER:]
 
     def update(turn, depth=NBR):
         @pl.when(space >= 0)
@@ -442,7 +460,8 @@
             keep(turn + 1, own[...] + apply(lhs_node, nbr_far, 0, depth))
 
     local_sums(0)
-    send_out(1, own_out[...])
+    for way in range(2):
+        send_one(1, way, own_out[way])
     for copy in far_copies:
         copy.wait_recv()
     side = jnp.where(iota((8, E), 1) < PEER, 0, 2 * PEER)
@@ -472,26 +491,45 @@
         extra[0, half * 8 : half * 8 + 8, :] = rows[:, :PEER]
         extra[1, half * 8 : half * 8 + 8, :] = rows[:, PEER:]
 
+    def near_part(way):
+        block = dot(table[:, LOCAL:], pick_near[way])
+        for face in range(6):
+            store_rows(nbr_near, face, oriented(block[:, face * PEER : face * PEER + PEER], turn_out[way, face]))
+
     def advance(turn, top_later=False):
         depth = K if top_later else NBR
         if not top_later:
             local_sums(turn)
         receive(turn, top_later)
-        remote_part(pick_near, 0, turn_out)
+        far_side = 1 - near_side
+        near_part(far_side)
         if top_later:
 
             @pl.when(space >= 0)
             def _():
-                own_out[...] += apply(lhs_node, nbr_far, 0, NBR)
+                own_out[far_side] = own_out[far_side] + apply(lhs_node, nbr_near, 0, NBR)
 
             take_top(turn, True)
 
         @pl.when(slab >= 0)
         def _():
-            begin, end = (NBR, K) if top_later else (0, NBR)
-            send_out(turn + 1, own_out[...] + apply(lhs_node, nbr_far, begin, end))
+            if top_later:
+                late = apply(lhs_node, nbr_far, NBR, K)
+                own_out[0] = own_out[0] + late[:, :PEER]
+                own_out[1] = own_out[1] + late[:, PEER:]
+                send_one(turn + 1, far_side, own_out[far_side])
+            else:
+                send_one(turn + 1, far_side, own_out[far_side] + apply(lhs_node, nbr_near, 0, NBR))
 
         update(turn, depth)
+
+        @pl.when(space >= 0)
+        def _():
+            near_part(near_side)
+
+        @pl.when(slab >= 0)
+        def _():
+            send_one(turn + 1, near_side, own_out[near_side] + apply(lhs_node, nbr_near, 0, NBR))
 
     advance(1, True)
 
@@ -543,7 +581,7 @@
             vmem((6, E), jnp.int32),
             vmem((1, E), jnp.int32),
             vmem((TABLE, LOCAL), BF16),
-            vmem((2 * PEER, LOCAL), BF16),
+            vmem((2, 2 * PEER, 6 * PEER), BF16),
             vmem((128, TABLE), BF16),
             vmem((K, E), BF16),
             vmem((K, E), BF16),
@@ -555,12 +593,14 @@
             vmem((256, 256), BF16),
             vmem((256, 256), BF16),
             vmem((256, E), F32),
-            vmem((256, E), F32),
+            vmem((2, 256, PEER), F32),
+            vmem((2, 8, PEER), jnp.int32),
+            vmem((NBR, PEER), BF16),
             vmem((256, 512), F32),
             vmem((512, K), BF16),
             vmem((16, LOCAL), jnp.int32),
             vmem((6, 8, E), jnp.int32),
-            vmem((6, 8, E), jnp.int32),
+            vmem((2, 6, 8, PEER), jnp.int32),
             vmem((32, E), F32),
             vmem((E, E), BF16),
             vmem((64, 8, E), F32),

time: 33 us -> 32.8 us (level)
  no operation moved by 1% of the time
where the time goes in v8:
time: 32.8 us; the launch traced here: 32.7 us
  Pallas kernels  31.3 us (95%)
  other arithmetic  0.73 us (2%)
  between operations  0.67 us (2%)
    pallas_call x1, Pallas kernels, body(): pl.pallas_call(functools.partial(kernel, n_space, n_slab), name='window',...  31.3 us
    select_n x1, other arithmetic, body(): return jnp.where(live[None, None, :], state, 0.0)  0.72 us

profile of v8, /device:TPU:6, one launch (start us, length us, event | category | flops | bytes accessed | tf_op | source)
XLA Modules:
  0.0 32.7 jit_solution(291887802484022262)
XLA Ops:
  0.7 31.3 %window.1 = f32[1,256,256]{2,1,0:T(8,128)S(1)} custom-call(f32[1,256,256]{2,1,0:T(8,128)} %source.1, f32[64,256]{1,0:T(8,128)} %initial.1, f32[256,256]{1,0:T(8,128)} %inverse.1, f32[256,384]{1,0:T(8,128)} %lift.1, f32[64,256]{1,0:T(8,128)} %bitcast.4, s32[6,256]{1,0:T(8,128)} %links.1, s32[6,256]{1,0:T(8,128)} %orient.1, s32[1,256]{1,0:T(1,128)} %bitcast.5), custom_call_target="tpu_custom_call" | custom-call | tf_op jit(solution)/shard_map/window/pallas_call | solution.py:568
  32.0 0.7 %broadcast_select_fusion = f32[1,256,256]{2,1,0:T(8,128)} fusion(f32[1,256,256]{2,1,0:T(8,128)S(1)} %window.1, pred[256]{0:T(512)(128)(4,1)S(1)} %iota_compare_fusion), kind=kLoop, calls=%fused_computation | loop fusion | flops 65536 | bytes 524544 | tf_op jit(solution)/shard_map/jit(_where)/select_n | solution.py:632
  (1 shorter events, 0.0 us)

commit v9 on v8

--- a/solution.py
+++ b/solution.py
@@ -168,6 +168,18 @@
     upper = {"space": lax.rem(space + 1, n_space)}
     lower = {"space": lax.rem(space + n_space - 1, n_space)}
 
+    barrier = pltpu.get_barrier_semaphore()
+    for peer in (lower, upper):
+        pl.semaphore_signal(barrier, inc=1, device_id=peer, device_id_type=MESH)
+
+    @pl.when(slab > 0)
+    def _():
+        pl.semaphore_signal(barrier, inc=1, device_id={"slab": slab - 1}, device_id_type=MESH)
+
+    @pl.when(slab < n_slab - 1)
+    def _():
+        pl.semaphore_signal(barrier, inc=1, device_id={"slab": slab + 1}, device_id_type=MESH)
+
     loads = []
     for at, (src, dst) in enumerate(
         (
@@ -185,18 +197,6 @@
         copy.start()
         loads.append(copy)
 
-    barrier = pltpu.get_barrier_semaphore()
-    for peer in (lower, upper):
-        pl.semaphore_signal(barrier, inc=1, device_id=peer, device_id_type=MESH)
-
-    @pl.when(slab > 0)
-    def _():
-        pl.semaphore_signal(barrier, inc=1, device_id={"slab": slab - 1}, device_id_type=MESH)
-
-    @pl.when(slab < n_slab - 1)
-    def _():
-        pl.semaphore_signal(barrier, inc=1, device_id={"slab": slab + 1}, device_id_type=MESH)
-
     def space_copies(turn):
         return [
             pltpu.make_async_remote_copy(
@@ -305,7 +305,7 @@
     nbr_far[NBR:, :] = jnp.zeros((128, E), BF16)
     lift_all[:, 384:] = jnp.zeros((E, 128), F32)
 
-    for load in loads[:6]:
+    for load in loads[:5]:
         load.wait()
     element = jnp.broadcast_to(v_exports[...] & 255, (E, E))
     select[...] = jnp.where(element == iota((E, E), 0), 1.0, 0.0).astype(BF16)
@@ -317,6 +317,7 @@
     time_high, time_low = halves(v_lift_time[...].T)
     first_high, first_low = halves(v_initial[...])
     start = dot(time_high, first_high) + dot(time_high, first_low) + dot(time_low, first_high)
+    loads[5].wait()
     inv_high, inv_low = halves(v_inverse[...])
     inv_node[:E, :] = dot(by_node[...], inv_high).astype(BF16)
     inv_node[E:, :] = dot(by_node[...], inv_low).astype(BF16)

time: 32.8 us -> 32.8 us (level)
  no operation moved by 1% of the time
where the time goes in v9:
time: 32.8 us; the launch traced here: 32.7 us
  Pallas kernels  31.3 us (95%)
  other arithmetic  0.73 us (2%)
  between operations  0.67 us (2%)
    pallas_call x1, Pallas kernels, body(): pl.pallas_call(functools.partial(kernel, n_space, n_slab), name='window',...  31.3 us
    select_n x1, other arithmetic, body(): return jnp.where(live[None, None, :], state, 0.0)  0.72 us

profile of v9, /device:TPU:6, one launch (start us, length us, event | category | flops | bytes accessed | tf_op | source)
XLA Modules:
  0.0 32.7 jit_solution(1682299757066308847)
XLA Ops:
  0.7 31.3 %window.1 = f32[1,256,256]{2,1,0:T(8,128)S(1)} custom-call(f32[1,256,256]{2,1,0:T(8,128)} %source.1, f32[64,256]{1,0:T(8,128)} %initial.1, f32[256,256]{1,0:T(8,128)} %inverse.1, f32[256,384]{1,0:T(8,128)} %lift.1, f32[64,256]{1,0:T(8,128)} %bitcast.4, s32[6,256]{1,0:T(8,128)} %links.1, s32[6,256]{1,0:T(8,128)} %orient.1, s32[1,256]{1,0:T(1,128)} %bitcast.5), custom_call_target="tpu_custom_call" | custom-call | tf_op jit(solution)/shard_map/window/pallas_call | solution.py:569
  31.9 0.7 %broadcast_select_fusion = f32[1,256,256]{2,1,0:T(8,128)} fusion(f32[1,256,256]{2,1,0:T(8,128)S(1)} %window.1, pred[256]{0:T(512)(128)(4,1)S(1)} %iota_compare_fusion), kind=kLoop, calls=%fused_computation | loop fusion | flops 65536 | bytes 524544 | tf_op jit(solution)/shard_map/jit(_where)/select_n | solution.py:633
  (1 shorter events, 0.0 us)
